TPU v7x, 32 devices: a 4x4x1 block of a 4x4x8 slice. The times are simulated.
32 devices in a mesh: rep: 1 (over z), dp: 32 (over x, y, core).
Axes of the slice: x: 4, y: 4, z: 1, core: 2. Of those that a mesh axis runs over, the one named last changes fastest.
The devices are a block of a 4x4x8 slice.
Arguments:
- g_w_gate: bfloat16 [32, 2, 1152, 4608], P(('rep', 'dp'))
- g_w_up: bfloat16 [32, 2, 1152, 4608], P(('rep', 'dp'))
- g_w_down: bfloat16 [32, 2, 4608, 1152], P(('rep', 'dp'))
- w_gate: bfloat16 [2, 1152, 4608], replicated
- w_up: bfloat16 [2, 1152, 4608], replicated
- w_down: bfloat16 [2, 4608, 1152], replicated
- m_w_gate: float32 [2, 1152, 4608], P(None, 'dp')
- m_w_up: float32 [2, 1152, 4608], P(None, 'dp')
- m_w_down: float32 [2, 4608, 1152], P(None, 'dp')
- v_w_gate: float32 [2, 1152, 4608], P(None, 'dp')
- v_w_up: float32 [2, 1152, 4608], P(None, 'dp')
- v_w_down: float32 [2, 4608, 1152], P(None, 'dp')
Outputs:
- output 1: bfloat16 [2, 1152, 4608], P('rep')
- output 2: bfloat16 [2, 1152, 4608], P('rep')
- output 3: bfloat16 [2, 4608, 1152], P('rep')
- output 4: float32 [2, 1152, 4608], P('rep', 'dp')
- output 5: float32 [2, 1152, 4608], P('rep', 'dp')
- output 6: float32 [2, 4608, 1152], P('rep', 'dp')
- output 7: float32 [2, 1152, 4608], P('rep', 'dp')
- output 8: float32 [2, 1152, 4608], P('rep', 'dp')
- output 9: float32 [2, 4608, 1152], P('rep', 'dp')
All inputs are finite; a program needn't handle non-finite values.
Results may differ from a plain program's by a relative error of at most 0.022.
Values are sent between devices in bfloat16 or wider.
A program may use at most 768 MiB of HBM per device.

v0:
```python
import jax
import jax.numpy as jnp
from jax import lax
from jax.sharding import PartitionSpec as P


def adamw(w, m, v, g):
    m = 0.9 * m + 0.1 * g
    v = 0.95 * v + 0.05 * g * g
    step = m * lax.rsqrt(v + 1e-8) + 0.1 * w
    return (w - 0.02 * step).astype(jnp.bfloat16), m, v


def solution(mesh):
    def step(*arrays):
        terms, weights, m, v = (arrays[i : i + 3] for i in (0, 3, 6, 9))
        gradients = [lax.psum_scatter(t[0], "dp", scatter_dimension=1, tiled=True).astype(jnp.float32) for t in terms]
        me = lax.axis_index("dp")
        own = [lax.dynamic_slice_in_dim(w, me * one.shape[1], one.shape[1], 1).astype(jnp.float32) for w, one in zip(weights, m, strict=True)]
        new = [adamw(w, m, v, g) for w, m, v, g in zip(own, m, v, gradients, strict=True)]
        whole = [lax.all_gather(one[0], "dp", axis=1, tiled=True) for one in new]
        return (*whole, *(one[1] for one in new), *(one[2] for one in new))

    all_of, cut = P(None, None, None), P(None, "dp", None)
    return jax.shard_map(
        step,
        mesh=mesh,
        in_specs=(P(("rep", "dp"), None, None, None),) * 3 + (all_of,) * 3 + (cut,) * 6,
        out_specs=(P("rep", None, None),) * 3 + (P("rep", "dp", None),) * 6,
        check_vma=False,
    )
```

profile of v0, /device:TPU:97, one launch (start us, length us, event | category | flops | bytes accessed | tf_op | source)
XLA Modules:
  0.0 846.8 jit_solution(6711088395283013137)
XLA Ops:
  7.2 0.1 all-reduce.5.cloned.1.call-start
  7.3 94.4 %copy.40 = bf16[1,2,1152,4608]{3,1,2,0:T(2,128)(2,1)} copy(bf16[1,2,1152,4608]{3,2,1,0:T(8,128)(2,1)} %param.12) | data formatting | bytes 42467328 | tf_op args[0]
  101.7 0.1 all-reduce.5.cloned.1.call-update
  101.8 0.1 all-reduce.7.cloned.1.call-start
  101.8 94.4 %copy.39 = bf16[1,2,1152,4608]{3,1,2,0:T(2,128)(2,1)} copy(bf16[1,2,1152,4608]{3,2,1,0:T(8,128)(2,1)} %param.13) | data formatting | bytes 42467328 | tf_op args[1]
  196.3 0.1 all-reduce.7.cloned.1.call-update
  196.3 0.1 reduce-scatter.2.cloned.1.call-start
  196.4 0.0 copy-start.3
  196.4 0.7 reduce-scatter.2.cloned.1.call-update
  197.1 0.0 copy-start.2
  197.1 0.1 all-gather.4.cloned.1.call-start
  197.2 1.4 constant_dynamic-slice_fusion.1
  198.7 84.0 %all-reduce.5.cloned.1.call-done = bf16[2,1152,4608]{2,0,1:T(2,128)(2,1)} async-done(((bf16[2,1152,4608]{2,0,1:T(2,128)(2,1)}), bf16[2,1152,4608]{2,0,1:T(2,128)(2,1)}) %all-reduce.5.cloned.1.call-update) | async-done | bytes 21233680
  282.6 0.0 copy-done.3
  282.6 0.0 copy-done.2
  282.7 6.0 fusion.13
  288.6 0.1 all-gather.4.cloned.1.call-update
  288.7 0.1 all-gather.6.cloned.1.call-start
  288.8 1.4 constant_dynamic-slice_fusion
  290.1 173.8 %all-reduce.7.cloned.1.call-done = bf16[2,1152,4608]{2,0,1:T(2,128)(2,1)} async-done(((bf16[2,1152,4608]{2,0,1:T(2,128)(2,1)}), bf16[2,1152,4608]{2,0,1:T(2,128)(2,1)}) %all-reduce.7.cloned.1.call-update) | async-done | bytes 21233680
  463.9 0.0 copy-start
  463.9 0.0 copy-start.1
  463.9 6.5 fusion.14
  470.4 0.1 all-gather.6.cloned.1.call-update
  470.4 0.2 all-gather.8.cloned.1.call-start
  470.7 111.3 %reduce-scatter.2.cloned.1.call-done = bf16[2,144,1152]{2,1,0:T(8,128)(2,1)} async-done(((bf16[2,4608,1152]{2,1,0:T(8,128)(2,1)}), bf16[2,144,1152]{2,1,0:T(8,128)(2,1)}) %reduce-scatter.2.cloned.1.call-update) | async-done | bytes 663568 | tf_op jit(solution)/shard_map/reduce_scatter | solution.py:17
  582.0 0.0 copy-done
  582.0 0.0 copy-done.1
  582.0 3.4 fusion.8
  585.4 0.1 all-gather.8.cloned.1.call-update
  585.4 78.3 %all-gather.4.cloned.1.call-done = bf16[2,1152,4608]{2,0,1:T(2,128)(2,1)} async-done(((bf16[2,36,4608]{2,0,1:T(2,128)(2,1)}), bf16[2,1152,4608]{2,0,1:T(2,128)(2,1)}) %all-gather.4.cloned.1.call-update) | async-done | bytes 21233680 | tf_op jit(solution)/shard_map/all_gather | solution.py:21
  663.7 19.5 %copy.31 = bf16[2,1152,4608]{2,1,0:T(8,128)(2,1)} copy(bf16[2,1152,4608]{2,0,1:T(2,128)(2,1)} %all-gather.4.cloned.1.call-done) | data formatting | bytes 42467328
  683.2 60.1 %all-gather.6.cloned.1.call-done = bf16[2,1152,4608]{2,0,1:T(2,128)(2,1)} async-done(((bf16[2,36,4608]{2,0,1:T(2,128)(2,1)}), bf16[2,1152,4608]{2,0,1:T(2,128)(2,1)}) %all-gather.6.cloned.1.call-update) | async-done | bytes 21233680 | tf_op jit(solution)/shard_map/all_gather | solution.py:21
  743.3 19.5 %copy.32 = bf16[2,1152,4608]{2,1,0:T(8,128)(2,1)} copy(bf16[2,1152,4608]{2,0,1:T(2,128)(2,1)} %all-gather.6.cloned.1.call-done) | data formatting | bytes 42467328
  762.8 59.6 %all-gather.8.cloned.1.call-done = bf16[2,4608,1152]{2,1,0:T(8,128)(2,1)} async-done(((bf16[2,144,1152]{2,1,0:T(8,128)(2,1)}), bf16[2,4608,1152]{2,1,0:T(8,128)(2,1)}) %all-gather.8.cloned.1.call-update) | async-done | bytes 21233680 | tf_op jit(solution)/shard_map/all_gather | solution.py:21
  822.5 17.4 %copy.44 = bf16[2,4608,1152]{2,1,0:T(8,128)(2,1)} copy(bf16[2,4608,1152]{2,1,0:T(8,128)(2,1)} %all-gather.8.cloned.1.call-done) | data formatting | bytes 42467328
Async XLA Ops:
  7.2 275.5 %all-reduce.5.cloned.1.call-start = ((), (), s32[]{:S(2)}) async-start(), calls=%async_computation.5 | async-start | bytes 42467328
  101.8 362.1 %all-reduce.7.cloned.1.call-start = ((), (), s32[]{:S(2)}) async-start(), calls=%async_computation.6 | async-start | bytes 42467328
  196.3 385.7 %reduce-scatter.2.cloned.1.call-start = ((), (), s32[]{:S(2)}) async-start(), calls=%async_computation.3 | async-start | bytes 21897216 | tf_op jit(solution)/shard_map/reduce_scatter | solution.py:17
  196.4 86.2 %copy-start.3 = (f32[2,36,4608]{2,0,1:T(2,128)S(1)}, f32[2,36,4608]{2,0,1:T(2,128)}, u32[]{:S(2)}) copy-start(f32[2,36,4608]{2,0,1:T(2,128)} %param.18) | copy-start | bytes 3981316
  197.1 85.5 %copy-start.2 = (f32[2,36,4608]{2,0,1:T(2,128)S(1)}, f32[2,36,4608]{2,0,1:T(2,128)}, u32[]{:S(2)}) copy-start(f32[2,36,4608]{2,0,1:T(2,128)} %param.21) | copy-start | bytes 3981316
  197.1 466.5 %all-gather.4.cloned.1.call-start = ((), (), s32[]{:S(2)}) async-start(), calls=%async_computation.1 | async-start | bytes 21897216 | tf_op jit(solution)/shard_map/all_gather | solution.py:21
  288.7 454.6 %all-gather.6.cloned.1.call-start = ((), (), s32[]{:S(2)}) async-start(), calls=%async_computation.2 | async-start | bytes 21897216 | tf_op jit(solution)/shard_map/all_gather | solution.py:21
  463.9 118.1 %copy-start = (f32[2,144,1152]{2,1,0:T(8,128)S(1)}, f32[2,144,1152]{2,1,0:T(8,128)}, u32[]{:S(2)}) copy-start(f32[2,144,1152]{2,1,0:T(8,128)} %param.23) | copy-start | bytes 3981316
  463.9 118.1 %copy-start.1 = (f32[2,144,1152]{2,1,0:T(8,128)S(1)}, f32[2,144,1152]{2,1,0:T(8,128)}, u32[]{:S(2)}) copy-start(f32[2,144,1152]{2,1,0:T(8,128)} %param.20) | copy-start | bytes 3981316
  470.4 352.1 %all-gather.8.cloned.1.call-start = ((), (), s32[]{:S(2)}) async-start(), calls=%async_computation.4 | async-start | bytes 21897216 | tf_op jit(solution)/shard_map/all_gather | solution.py:21
Sparse Core Ops, SparseCore 0:
  101.9 180.7 all-reduce.4
  287.0 176.8 all-reduce.6
  467.8 114.1 reduce-scatter.1
  584.5 79.1 all-gather.3
  666.2 77.0 all-gather.5
  745.4 77.0 all-gather.7
where the time goes:
time: 847 us
  waiting for transfers between devices  568 us (67%)
  local copies, waits for them, and re-layouts  248 us (29%)
  other arithmetic  15.8 us (2%)
  between operations  14.2 us (2%)
    unnamed x8, waiting for transfers between devices  259 us
    unnamed x13, local copies, waits for them, and re-layouts  245 us
    all_gather x3, waiting for transfers between devices, step(): whole = [lax.all_gather(one[0], 'dp', axis=1, tiled=True) for one in new]  198 us
    reduce_scatter x1, waiting for transfers between devices, step(): lax.psum_scatter(t[0], 'dp', scatter_dimension=1, tiled=True)  111 us
  transfers between devices with their start and end apart: 6, of which 6 were waited for; matrix products, arithmetic and copies ran while one was open for 18% of the time, Pallas kernels for 0%

commit v1 on v0

v1 whole, which is shorter than its diff:
```python
import functools
import math

import jax
import jax.numpy as jnp
from jax import lax
from jax.experimental import pallas as pl
from jax.experimental.pallas import tpu as pltpu
from jax.sharding import PartitionSpec as P

MESH = pl.DeviceIdType.MESH
F32, BF16 = jnp.float32, jnp.bfloat16
SLOTS = 4
HOLD = 3


def adamw(w, m, v, g):
    m = 0.9 * m + 0.1 * g
    v = 0.95 * v + 0.05 * g * g
    step = m * lax.rsqrt(v + 1e-8) + 0.1 * w
    return (w - 0.02 * step).astype(BF16), m, v


class Place:
    def __init__(self, side):
        me = lax.axis_index("dp")
        self.side = side
        self.core = me % 2
        chip = me // 2
        x, y = chip // side, chip % side
        self.chip = chip
        self.f = x + self.core * (y - x)
        self.s = y + self.core * (x - y)
        self.mf = side - (side - 1) * self.core
        self.ms = 1 + (side - 1) * self.core

    def device(self, df, ds):
        f, s = (self.f + df) % self.side, (self.s + ds) % self.side
        return {"dp": (f * self.mf + s * self.ms) * 2 + self.core}

    def partner(self):
        return {"dp": self.chip * 2 + 1 - self.core}

    def around(self):
        d = self.side - 1
        return [self.device(1, 0), self.device(d, 0), self.device(0, 1), self.device(0, d), self.partner()]

    def greet(self):
        barrier = pltpu.get_barrier_semaphore()
        others = self.around()
        for other in others:
            pl.semaphore_signal(barrier, inc=1, device_id=other, device_id_type=MESH)
        pl.semaphore_wait(barrier, len(others))


def send(src, dst, send_sem, recv_sem, device):
    return pltpu.make_async_remote_copy(
        src_ref=src, dst_ref=dst, send_sem=send_sem, recv_sem=recv_sem, device_id=device, device_id_type=MESH
    )


def wait_for(ref, sem):
    pltpu.make_async_copy(ref, ref, sem).wait()


def reduce_kernel(side, quarters, rows, cols, *refs):
    terms = refs[:3]
    out = refs[3]
    (own, par, ra, rb, fl, fr, hold, sums, ra2, rb2, fl2, fr2, g) = refs[4:17]
    (own_sem, par_send, par_sem, a_send, ra_sem, rb_sem, fl_sem, fr_sem, s_send, ra2_sem, rb2_sem, fl2_sem, fr2_sem, g_send, g_sem, out_sem, credit) = refs[17:]
    pieces = 3 * quarters
    half = side // 2
    top = (rows // 2 + 7) // 8 * 8
    at = Place(side)
    core, f, s = at.core, at.f, at.s
    last = side - 1
    right, left = at.device(1, 0), at.device(last, 0)
    up, down = at.device(0, 1), at.device(0, last)
    partner = at.partner()
    fp, fm, f2 = (f + 1) % side, (f + last) % side, (f + 2) % side
    sp, sm, s2 = (s + 1) % side, (s + last) % side, (s + 2) % side
    at.greet()

    def block(which, layer, quarter, chip):
        ref = terms[which]
        if which < 2:
            return ref.at[0, layer, pl.ds(pl.multiple_of(chip * rows, 8), rows), pl.ds(pl.multiple_of(quarter * cols, 128), cols)]
        return ref.at[0, layer, pl.ds(pl.multiple_of((chip * quarters + quarter) * rows, 8), rows), :]

    def load(i):
        slot = i % SLOTS
        for which in range(3):

            @pl.when(i // quarters == which)
            def _(which=which):
                @pl.loop(0, side * side)
                def _(n):
                    bf, bs = n // side, n % side
                    send(
                        block(which, 1 - core, i % quarters, bf * at.ms + bs * at.mf),
                        par.at[slot, bf, bs],
                        par_send.at[slot],
                        par_sem.at[slot],
                        partner,
                    ).start()
                    pltpu.make_async_copy(
                        block(which, core, i % quarters, bf * at.mf + bs * at.ms), own.at[slot, bf, bs], own_sem.at[slot]
                    ).start()

    def pair(slot, bf, bs):
        return own[slot, bf, bs].astype(F32) + par[slot, bf, bs].astype(F32)

    load(0)
    load(1)

    @pl.loop(0, pieces + 4)
    def _(t):
        @pl.when(t < pieces)
        def _():
            i, slot = t, t % SLOTS
            wait_for(own.at[slot], own_sem.at[slot])
            wait_for(par.at[slot], par_sem.at[slot])

            @pl.loop(0, side)
            def _(n):
                own[slot, f2, n] = pair(slot, f2, n).astype(BF16)

            send(own.at[slot, f2, pl.ds(0, half)], ra.at[i], a_send.at[slot], ra_sem.at[i], right).start()
            send(own.at[slot, f2, pl.ds(half, half)], rb.at[i], a_send.at[slot], rb_sem.at[i], left).start()

            @pl.loop(0, half)
            def _(n):
                own[slot, fp, half + n] = pair(slot, fp, half + n).astype(BF16)
                own[slot, fm, n] = pair(slot, fm, n).astype(BF16)

            send(own.at[slot, fp, pl.ds(half, half)], fl.at[i, pl.ds(half, half)], a_send.at[slot], fl_sem.at[i], right).start()
            send(own.at[slot, fm, pl.ds(0, half)], fr.at[i, pl.ds(0, half)], a_send.at[slot], fr_sem.at[i], left).start()

        @pl.when((t >= 1) & (t < pieces + 1))
        def _():
            i = t - 1
            slot = i % SLOTS
            wait_for(ra.at[i], ra_sem.at[i])
            wait_for(rb.at[i], rb_sem.at[i])

            @pl.loop(0, half)
            def _(n):
                own[slot, fp, n] = (pair(slot, fp, n) + ra[i, n].astype(F32)).astype(BF16)
                own[slot, fm, half + n] = (pair(slot, fm, half + n) + rb[i, n].astype(F32)).astype(BF16)

            send(own.at[slot, fp, pl.ds(0, half)], fl.at[i, pl.ds(0, half)], a_send.at[slot], fl_sem.at[i], right).start()
            send(own.at[slot, fm, pl.ds(half, half)], fr.at[i, pl.ds(half, half)], a_send.at[slot], fr_sem.at[i], left).start()

        @pl.when((t >= 2) & (t < pieces + 2))
        def _():
            i = t - 2
            slot, h = i % SLOTS, i % HOLD

            @pl.when(i >= HOLD)
            def _():
                wait_for(sums.at[h, pl.ds(0, last)], s_send.at[h])

            wait_for(fl.at[i], fl_sem.at[i])
            wait_for(fr.at[i], fr_sem.at[i])

            @pl.loop(0, side)
            def _(n):
                total = pair(slot, f, n) + fl[i, n].astype(F32) + fr[i, n].astype(F32)
                hold[h, n] = total
                sums[h, n] = total.astype(BF16)

            send(sums.at[h, s2, pl.ds(0, top)], ra2.at[i], s_send.at[h], ra2_sem.at[i], up).start()
            send(sums.at[h, s2, pl.ds(top, rows - top)], rb2.at[i], s_send.at[h], rb2_sem.at[i], down).start()
            send(sums.at[h, sp, pl.ds(top, rows - top)], fl2.at[i, pl.ds(top, rows - top)], s_send.at[h], fl2_sem.at[i], up).start()
            send(sums.at[h, sm, pl.ds(0, top)], fr2.at[i, pl.ds(0, top)], s_send.at[h], fr2_sem.at[i], down).start()

            @pl.when(i + SLOTS < pieces)
            def _():
                pl.semaphore_signal(credit, inc=1, device_id=partner, device_id_type=MESH)

        @pl.when(t + 2 < pieces)
        def _():
            @pl.when(t + 2 >= SLOTS)
            def _():
                slot = (t + 2) % SLOTS
                wait_for(own.at[slot, pl.ds(0, last)], a_send.at[slot])
                wait_for(own.at[slot], par_send.at[slot])
                pl.semaphore_wait(credit, 1)

            load(t + 2)

        @pl.when((t >= 3) & (t < pieces + 3))
        def _():
            i = t - 3
            h = i % HOLD
            wait_for(ra2.at[i], ra2_sem.at[i])
            wait_for(rb2.at[i], rb2_sem.at[i])
            sums[h, sp, pl.ds(0, top)] = (hold[h, sp, pl.ds(0, top)] + ra2[i].astype(F32)).astype(BF16)
            sums[h, sm, pl.ds(top, rows - top)] = (hold[h, sm, pl.ds(top, rows - top)] + rb2[i].astype(F32)).astype(BF16)
            send(sums.at[h, sp, pl.ds(0, top)], fl2.at[i, pl.ds(0, top)], s_send.at[h], fl2_sem.at[i], up).start()
            send(sums.at[h, sm, pl.ds(top, rows - top)], fr2.at[i, pl.ds(top, rows - top)], s_send.at[h], fr2_sem.at[i], down).start()

        @pl.when(t >= 4)
        def _():
            i = t - 4
            h = i % HOLD
            wait_for(fl2.at[i], fl2_sem.at[i])
            wait_for(fr2.at[i], fr2_sem.at[i])
            g[i, core] = (hold[h, s] + fl2[i].astype(F32) + fr2[i].astype(F32)).astype(BF16)
            send(g.at[i, core], g.at[i, core], g_send.at[i], g_sem.at[i], partner).start()

    @pl.loop(0, pieces)
    def _(i):
        wait_for(g.at[i, core], g_sem.at[i])
        pltpu.make_async_copy(g.at[i], out.at[i], out_sem.at[i]).start()

    for n in range(SLOTS):
        slot = (pieces + n) % SLOTS
        wait_for(own.at[slot, pl.ds(0, last)], a_send.at[slot])
        wait_for(own.at[slot], par_send.at[slot])
    for n in range(HOLD):
        wait_for(sums.at[n, pl.ds(0, last)], s_send.at[n])

    @pl.loop(0, pieces)
    def _(i):
        wait_for(g.at[i, core], g_send.at[i])
        pltpu.make_async_copy(g.at[i], out.at[i], out_sem.at[i]).wait()


def reduce_scatter(terms, side):
    _, layers, d, ff = terms[0].shape
    quarters = ff // d
    rows, cols = d // (side * side), d
    pieces = 3 * quarters
    if side != 4 or layers != 2:
        raise ValueError("wrong sizes")
    top = (rows // 2 + 7) // 8 * 8
    dma = pltpu.SemaphoreType.DMA
    any_ = pl.BlockSpec(memory_space=pl.ANY)
    return pl.pallas_call(
        functools.partial(reduce_kernel, side, quarters, rows, cols),
        out_shape=jax.ShapeDtypeStruct((pieces, layers, rows, cols), BF16),
        in_specs=[any_] * 3,
        out_specs=any_,
        scratch_shapes=[
            pltpu.VMEM((SLOTS, side, side, rows, cols), BF16),
            pltpu.VMEM((SLOTS, side, side, rows, cols), BF16),
            pltpu.VMEM((pieces, side // 2, rows, cols), BF16),
            pltpu.VMEM((pieces, side // 2, rows, cols), BF16),
            pltpu.VMEM((pieces, side, rows, cols), BF16),
            pltpu.VMEM((pieces, side, rows, cols), BF16),
            pltpu.VMEM((HOLD, side, rows, cols), F32),
            pltpu.VMEM((HOLD, side, rows, cols), BF16),
            pltpu.VMEM((pieces, top, cols), BF16),
            pltpu.VMEM((pieces, rows - top, cols), BF16),
            pltpu.VMEM((pieces, rows, cols), BF16),
            pltpu.VMEM((pieces, rows, cols), BF16),
            pltpu.VMEM((pieces, layers, rows, cols), BF16),
            dma((SLOTS,)),
            dma((SLOTS,)),
            dma((SLOTS,)),
            dma((SLOTS,)),
            dma((pieces,)),
            dma((pieces,)),
            dma((pieces,)),
            dma((pieces,)),
            dma((HOLD,)),
            dma((pieces,)),
            dma((pieces,)),
            dma((pieces,)),
            dma((pieces,)),
            dma((pieces,)),
            dma((pieces,)),
            dma((pieces,)),
            pltpu.SemaphoreType.REGULAR,
        ],
        compiler_params=pltpu.CompilerParams(collective_id=0, has_side_effects=True, vmem_limit_bytes=67043328),
        name="reduce_scatter",
    )(*terms)


def solution(mesh):
    side = math.isqrt(mesh.shape["dp"] // 2)

    def step(*arrays):
        terms, weights, m, v = (arrays[i : i + 3] for i in (0, 3, 6, 9))
        me = lax.axis_index("dp")
        quarters = terms[0].shape[3] // terms[0].shape[2]
        pieces = reduce_scatter(terms, side)
        gradients = []
        for n in range(3):
            part = pieces[n * quarters : (n + 1) * quarters]
            part = part.transpose(1, 2, 0, 3) if n < 2 else part.transpose(1, 0, 2, 3)
            part = part.reshape(part.shape[0], -1, weights[n].shape[2])
            own = m[n].shape[1]
            gradients.append(lax.dynamic_slice_in_dim(part, me % 2 * own, own, 1).astype(F32))
        own = [lax.dynamic_slice_in_dim(w, me * one.shape[1], one.shape[1], 1).astype(F32) for w, one in zip(weights, m, strict=True)]
        new = [adamw(w, m, v, g) for w, m, v, g in zip(own, m, v, gradients, strict=True)]
        whole = [lax.all_gather(one[0], "dp", axis=1, tiled=True) for one in new]
        return (*whole, *(one[1] for one in new), *(one[2] for one in new))

    all_of, cut = P(None, None, None), P(None, "dp", None)
    return jax.shard_map(
        step,
        mesh=mesh,
        in_specs=(P(("rep", "dp"), None, None, None),) * 3 + (all_of,) * 3 + (cut,) * 6,
        out_specs=(P("rep", None, None),) * 3 + (P("rep", "dp", None),) * 6,
        check_vma=False,
    )
```

time: 847 us -> 468 us (0.55)
  waiting for transfers between devices: 568 us -> 193 us
  Pallas kernels: 0 us -> 183 us
  local copies, waits for them, and re-layouts: 248 us -> 68 us
    unnamed x8 -> x3, waiting for transfers between devices: 259 us -> 0.16 us
    unnamed x13 -> x11, local copies, waits for them, and re-layouts: 245 us -> 58.2 us
    pallas_call x0 -> x1, Pallas kernels: none -> 183 us  [reduce_scatter(): pl.pallas_call(functools.partial(reduce_kernel, side, quarters, rows, col...]
    reduce_scatter x1 -> x0, waiting for transfers between devices: 111 us -> none  [step(): lax.psum_scatter(t[0], 'dp', scatter_dimension=1, tiled=True)]
  transfers between devices with their start and end apart: 6 -> 3, of which waited for: 6 -> 3; matrix products, arithmetic and copies ran while one was open for 18% -> 9% of each run, Pallas kernels for 0% -> 0%
where the time goes in v1:
time: 468 us
  waiting for transfers between devices  193 us (41%)
  Pallas kernels  183 us (39%)
  local copies, waits for them, and re-layouts  68 us (15%)
  between operations  13.8 us (3%)
  other arithmetic  9.97 us (2%)
    all_gather x3, waiting for transfers between devices, step(): whole = [lax.all_gather(one[0], 'dp', axis=1, tiled=True) for one in new]  193 us
    pallas_call x1, Pallas kernels, reduce_scatter(): pl.pallas_call(functools.partial(reduce_kernel, side, quarters, rows, col...  183 us
    unnamed x11, local copies, waits for them, and re-layouts  58.2 us
    convert_element_type x2, other arithmetic, adamw(): return ((w - 0.02 * step).astype(BF16), m, v)  9.97 us
  transfers between devices with their start and end apart: 3, of which 3 were waited for; matrix products, arithmetic and copies ran while one was open for 9% of the time, Pallas kernels for 0%

profile of v1, /device:TPU:97, one launch (start us, length us, event | category | flops | bytes accessed | tf_op | source)
XLA Modules:
  0.0 467.8 jit_solution(3811394731627847802)
XLA Ops:
  7.2 0.1 all-gather.8.cloned.1.call-start
  7.3 182.7 %reduce_scatter.1 = bf16[12,2,72,1152]{3,2,1,0:T(8,128)(2,1)} custom-call(bf16[1,2,1152,4608]{3,2,1,0:T(8,128)(2,1)} %refs_0_.1, bf16[1,2,1152,4608]{3,2,1,0:T(8,128)(2,1)} %refs_1_.1, bf16[1,2,4608,1152]{3,2,1,0:T(8,128)(2,1)} %refs_2_.1), custom_call_target="tpu_custom_call" | custom-call | tf_op jit(solution)/shard_map/reduce_scatter/pallas_call | solution.py:240
  190.0 2.4 slice_bitcast_fusion
  192.4 1.2 copy.44
  193.6 4.2 fusion.12
  197.8 0.1 all-gather.8.cloned.1.call-update
  197.8 0.1 all-gather.4.cloned.1.call-start
  197.9 1.2 copy.52
  199.1 1.2 copy.51
  200.3 5.8 %fusion.2 = (bf16[2,36,4608]{2,1,0:T(8,128)(2,1)S(1)}, f32[2,36,4608]{2,1,0:T(8,128)}, f32[2,36,4608]{2,1,0:T(8,128)}, bf16[2,36,4608]{2,1,0:T(8,128)(2,1)}, f32...) fusion(bf16[2,1152,4608]{2,1,0:T(8,128)(2,1)} %param.15, s32[]{:T(128)S(6)} %select_n.25, ...), kind=kLoop, calls=%fused_computation.14 | loop fusion | flops 10616832 | bytes 14598152 | tf_op jit(solution)/shard_map/convert_element_type | solution.py:21
  206.0 1.4 copy.39
  207.4 0.1 all-gather.4.cloned.1.call-update
  207.4 0.2 all-gather.6.cloned.1.call-start
  207.7 2.5 copy.43
  210.2 0.1 all-gather.6.cloned.1.call-update
  210.2 0.0 copy-start.1
  210.3 3.6 copy.49
  213.8 0.0 copy-done.1
  213.8 2.1 copy.47
  215.9 2.1 copy.50
  218.0 2.1 copy.48
  220.1 53.4 %all-gather.8.cloned.1.call-done = bf16[2,4608,1152]{2,1,0:T(8,128)(2,1)} async-done(((bf16[2,144,1152]{2,1,0:T(8,128)(2,1)}), bf16[2,4608,1152]{2,1,0:T(8,128)(2,1)}) %all-gather.8.cloned.1.call-update) | async-done | bytes 21233680 | tf_op jit(solution)/shard_map/all_gather | solution.py:299
  273.4 79.8 %all-gather.4.cloned.1.call-done = bf16[2,1152,4608]{2,0,1:T(2,128)(2,1)} async-done(((bf16[2,36,4608]{2,0,1:T(2,128)(2,1)}), bf16[2,1152,4608]{2,0,1:T(2,128)(2,1)}) %all-gather.4.cloned.1.call-update) | async-done | bytes 21233680 | tf_op jit(solution)/shard_map/all_gather | solution.py:299
  353.2 19.5 %copy.45 = bf16[2,1152,4608]{2,1,0:T(8,128)(2,1)} copy(bf16[2,1152,4608]{2,0,1:T(2,128)(2,1)} %all-gather.4.cloned.1.call-done) | data formatting | bytes 42467328
  372.8 59.7 %all-gather.6.cloned.1.call-done = bf16[2,1152,4608]{2,0,1:T(2,128)(2,1)} async-done(((bf16[2,36,4608]{2,0,1:T(2,128)(2,1)}), bf16[2,1152,4608]{2,0,1:T(2,128)(2,1)}) %all-gather.6.cloned.1.call-update) | async-done | bytes 21233680 | tf_op jit(solution)/shard_map/all_gather | solution.py:299
  432.5 0.0 copy-start
  432.5 21.2 %copy.46 = bf16[2,1152,4608]{2,1,0:T(8,128)(2,1)} copy(bf16[2,1152,4608]{2,0,1:T(2,128)(2,1)} %all-gather.6.cloned.1.call-done) | data formatting | bytes 42467328
  453.6 0.0 copy-done
  453.6 7.6 %copy.70 = bf16[2,4608,1152]{2,1,0:T(8,128)(2,1)} copy(bf16[2,4608,1152]{2,1,0:T(8,128)(2,1)S(1)} %copy-done) | data formatting | bytes 42467328
Async XLA Ops:
  7.2 266.3 %all-gather.8.cloned.1.call-start = ((), (), s32[]{:S(2)}) async-start(), calls=%async_computation.2 | async-start | bytes 21897216 | tf_op jit(solution)/shard_map/all_gather | solution.py:299
  197.8 155.4 %all-gather.4.cloned.1.call-start = ((), (), s32[]{:S(2)}) async-start(), calls=%async_computation | async-start | bytes 21897216 | tf_op jit(solution)/shard_map/all_gather | solution.py:299
  207.4 225.0 %all-gather.6.cloned.1.call-start = ((), (), s32[]{:S(2)}) async-start(), calls=%async_computation.1 | async-start | bytes 21897216 | tf_op jit(solution)/shard_map/all_gather | solution.py:299
  210.2 3.6 copy-start.1
  432.5 21.2 %copy-start = (bf16[2,4608,1152]{2,1,0:T(8,128)(2,1)S(1)}, bf16[2,4608,1152]{2,1,0:T(8,128)(2,1)}, u32[]{:S(2)}) copy-start(bf16[2,4608,1152]{2,1,0:T(8,128)(2,1)} %all-gather.8.cloned.1.call-done) | copy-start | bytes 63700996
Sparse Core Ops, SparseCore 0:
  197.9 75.4 all-gather.7
  276.1 77.0 all-gather.3
  355.3 77.0 all-gather.5

commit v2 on v1

v2 whole, which is shorter than its diff:
```python
import functools
import math

import jax
import jax.numpy as jnp
from jax import lax
from jax.experimental import pallas as pl
from jax.experimental.pallas import tpu as pltpu
from jax.sharding import PartitionSpec as P


MESH = pl.DeviceIdType.MESH
F32, BF16 = jnp.float32, jnp.bfloat16
SLOTS = 4
HOLD = 3
RING_A, RING_F = 4, 6


def adamw(w, m, v, g):
    m = 0.9 * m + 0.1 * g
    v = 0.95 * v + 0.05 * g * g
    step = m * lax.rsqrt(v + 1e-8) + 0.1 * w
    return (w - 0.02 * step).astype(BF16), m, v


class Place:
    def __init__(self, side):
        me = lax.axis_index("dp")
        self.side = side
        self.core = me % 2
        chip = me // 2
        x, y = chip // side, chip % side
        self.chip = chip
        self.f = x + self.core * (y - x)
        self.s = y + self.core * (x - y)
        self.mf = side - (side - 1) * self.core
        self.ms = 1 + (side - 1) * self.core

    def device(self, df, ds):
        f, s = (self.f + df) % self.side, (self.s + ds) % self.side
        return {"dp": (f * self.mf + s * self.ms) * 2 + self.core}

    def partner(self):
        return {"dp": self.chip * 2 + 1 - self.core}

    def around(self):
        d = self.side - 1
        return [self.device(1, 0), self.device(d, 0), self.device(0, 1), self.device(0, d), self.partner()]

    def greet(self):
        barrier = pltpu.get_barrier_semaphore()
        others = self.around()
        for other in others:
            pl.semaphore_signal(barrier, inc=1, device_id=other, device_id_type=MESH)
        pl.semaphore_wait(barrier, len(others))


def send(src, dst, send_sem, recv_sem, device):
    return pltpu.make_async_remote_copy(
        src_ref=src, dst_ref=dst, send_sem=send_sem, recv_sem=recv_sem, device_id=device, device_id_type=MESH
    )


def wait_for(ref, sem):
    pltpu.make_async_copy(ref, ref, sem).wait()


def reduce_kernel(side, quarters, rows, cols, *refs):
    terms, weights, ms, vs = (refs[n : n + 3] for n in (0, 3, 6, 9))
    out, units = refs[12], refs[13:17]
    (own, par, ra, rb, fl, fr, hold, sums, ra2, rb2, fl2, fr2, g, mv_own, mv_par, mv_down, w_old, w_new) = refs[17:35]
    (own_sem, par_send, par_sem, a_send, ra_sem, rb_sem, fl_sem, fr_sem, s_send, ra2_sem, rb2_sem, fl2_sem, fr2_sem, g_send, g_sem, out_sem) = refs[35:51]
    (w_sem, mv_sem, mp_sem, mp_send, n_send, n_own, nl_sem, nr_sem, no_sem, f_send, credit) = refs[51:]
    pieces = 3 * quarters
    wide = 2 * quarters
    half = side // 2
    top = (rows // 2 + 7) // 8 * 8
    at = Place(side)
    core, f, s = at.core, at.f, at.s
    last = side - 1
    right, left = at.device(1, 0), at.device(last, 0)
    up, down = at.device(0, 1), at.device(0, last)
    partner = at.partner()
    fp, fm, f2 = (f + 1) % side, (f + last) % side, (f + 2) % side
    sp, sm, s2 = (s + 1) % side, (s + last) % side, (s + 2) % side
    at.greet()

    def columns(quarter):
        return pl.ds(pl.multiple_of(quarter * cols, 128), cols)

    def block(refs, which, lead, layer, quarter, chip):
        ref = refs[which]
        if which < 2:
            return ref.at[*lead, layer, pl.ds(pl.multiple_of(chip * rows, 8), rows), columns(quarter)]
        return ref.at[*lead, layer, pl.ds(pl.multiple_of((chip * quarters + quarter) * rows, 8), rows), :]

    def each(i, do):
        for which in range(3):

            @pl.when(i // quarters == which)
            def _(which=which):
                do(which, i % quarters)

    def load(i):
        slot = i % SLOTS

        def do(which, quarter):
            @pl.loop(0, side * side)
            def _(n):
                bf, bs = n // side, n % side
                send(
                    block(terms, which, (0,), 1 - core, quarter, bf * at.ms + bs * at.mf),
                    par.at[slot, bf, bs],
                    par_send.at[slot],
                    par_sem.at[slot],
                    partner,
                ).start()
                pltpu.make_async_copy(
                    block(terms, which, (0,), core, quarter, bf * at.mf + bs * at.ms), own.at[slot, bf, bs], own_sem.at[slot]
                ).start()

        each(i, do)

    def load_state(i):
        def do(which, quarter):
            pltpu.make_async_copy(block(weights, which, (), core, quarter, at.chip), w_old.at[i], w_sem.at[i]).start()
            for n, ref in enumerate((ms[which], vs[which])):
                if which < 2:
                    part = ref.at[:, :, columns(quarter)]
                    pltpu.make_async_copy(part, mv_own.at[i, n], mv_sem.at[i]).start()
                    send(part, mv_par.at[i, n], mp_send.at[i], mp_sem.at[i], partner).start()
                else:

                    @pl.when(quarter // half == core)
                    def _(n=n, ref=ref):
                        here = pl.ds(pl.multiple_of(quarter % half * rows, 8), rows)
                        pltpu.make_async_copy(ref.at[core, here], mv_down.at[quarter, n], mv_sem.at[i]).start()
                        send(ref.at[1 - core, here], mv_down.at[quarter, n], mp_send.at[i], mp_sem.at[i], partner).start()

        each(i, do)

    def unit(i, do):
        for n in range(2):

            @pl.when(i // quarters == n)
            def _(n=n):
                do(lambda bf, at_row, size: units[n].at[bf, pl.ds(at_row, size), columns(i % quarters)])

        for n in range(2):

            @pl.when((i >= wide) & ((i - wide) // half == n))
            def _(n=n):
                start = pl.multiple_of(i % half * rows, 8)
                do(lambda bf, at_row, size: units[2 + n].at[bf, pl.ds(start + at_row, size), :])

    def pair(slot, bf, bs):
        return own[slot, bf, bs].astype(F32) + par[slot, bf, bs].astype(F32)

    load(0)
    load(1)

    @pl.loop(0, pieces + 5)
    def _(t):
        @pl.when(t < pieces)
        def _():
            i, slot = t, t % SLOTS
            a, b = i % RING_A, i % RING_F
            wait_for(own.at[slot], own_sem.at[slot])
            wait_for(par.at[slot], par_sem.at[slot])

            @pl.loop(0, side)
            def _(n):
                own[slot, f2, n] = pair(slot, f2, n).astype(BF16)

            send(own.at[slot, f2, pl.ds(0, half)], ra.at[a], a_send.at[slot], ra_sem.at[a], right).start()
            send(own.at[slot, f2, pl.ds(half, half)], rb.at[a], a_send.at[slot], rb_sem.at[a], left).start()

            @pl.loop(0, half)
            def _(n):
                own[slot, fp, half + n] = pair(slot, fp, half + n).astype(BF16)
                own[slot, fm, n] = pair(slot, fm, n).astype(BF16)

            send(own.at[slot, fp, pl.ds(half, half)], fl.at[b, pl.ds(half, half)], a_send.at[slot], fl_sem.at[b], right).start()
            send(own.at[slot, fm, pl.ds(0, half)], fr.at[b, pl.ds(0, half)], a_send.at[slot], fr_sem.at[b], left).start()

        @pl.when((t >= 1) & (t < pieces + 1))
        def _():
            i = t - 1
            slot, a, b = i % SLOTS, i % RING_A, i % RING_F
            wait_for(ra.at[a], ra_sem.at[a])
            wait_for(rb.at[a], rb_sem.at[a])

            @pl.loop(0, half)
            def _(n):
                own[slot, fp, n] = (pair(slot, fp, n) + ra[a, n].astype(F32)).astype(BF16)
                own[slot, fm, half + n] = (pair(slot, fm, half + n) + rb[a, n].astype(F32)).astype(BF16)

            send(own.at[slot, fp, pl.ds(0, half)], fl.at[b, pl.ds(0, half)], a_send.at[slot], fl_sem.at[b], right).start()
            send(own.at[slot, fm, pl.ds(half, half)], fr.at[b, pl.ds(half, half)], a_send.at[slot], fr_sem.at[b], left).start()

        @pl.when((t >= 2) & (t < pieces + 2))
        def _():
            i = t - 2
            slot, h, a, b = i % SLOTS, i % HOLD, i % RING_A, i % RING_F

            @pl.when(i >= HOLD)
            def _():
                wait_for(sums.at[h, pl.ds(0, last)], s_send.at[h])

            wait_for(fl.at[b], fl_sem.at[b])
            wait_for(fr.at[b], fr_sem.at[b])

            @pl.loop(0, side)
            def _(n):
                total = pair(slot, f, n) + fl[b, n].astype(F32) + fr[b, n].astype(F32)
                hold[h, n] = total
                sums[h, n] = total.astype(BF16)

            send(sums.at[h, s2, pl.ds(0, top)], ra2.at[a], s_send.at[h], ra2_sem.at[a], up).start()
            send(sums.at[h, s2, pl.ds(top, rows - top)], rb2.at[a], s_send.at[h], rb2_sem.at[a], down).start()
            send(sums.at[h, sp, pl.ds(top, rows - top)], fl2.at[b, pl.ds(top, rows - top)], s_send.at[h], fl2_sem.at[b], up).start()
            send(sums.at[h, sm, pl.ds(0, top)], fr2.at[b, pl.ds(0, top)], s_send.at[h], fr2_sem.at[b], down).start()

            @pl.when(i + SLOTS < pieces)
            def _():
                pl.semaphore_signal(credit, inc=1, device_id=partner, device_id_type=MESH)

        @pl.when(t + 2 < pieces)
        def _():
            @pl.when(t + 2 >= SLOTS)
            def _():
                slot = (t + 2) % SLOTS
                wait_for(own.at[slot, pl.ds(0, last)], a_send.at[slot])
                wait_for(own.at[slot], par_send.at[slot])
                pl.semaphore_wait(credit, 1)

            load(t + 2)

        @pl.when(t < pieces)
        def _():
            load_state(t)

        @pl.when((t >= 3) & (t < pieces + 3))
        def _():
            i = t - 3
            h, a, b = i % HOLD, i % RING_A, i % RING_F
            wait_for(ra2.at[a], ra2_sem.at[a])
            wait_for(rb2.at[a], rb2_sem.at[a])
            sums[h, sp, pl.ds(0, top)] = (hold[h, sp, pl.ds(0, top)] + ra2[a].astype(F32)).astype(BF16)
            sums[h, sm, pl.ds(top, rows - top)] = (hold[h, sm, pl.ds(top, rows - top)] + rb2[a].astype(F32)).astype(BF16)
            send(sums.at[h, sp, pl.ds(0, top)], fl2.at[b, pl.ds(0, top)], s_send.at[h], fl2_sem.at[b], up).start()
            send(sums.at[h, sm, pl.ds(top, rows - top)], fr2.at[b, pl.ds(top, rows - top)], s_send.at[h], fr2_sem.at[b], down).start()

        @pl.when((t >= 4) & (t < pieces + 4))
        def _():
            i = t - 4
            h, b = i % HOLD, i % RING_F
            wait_for(fl2.at[b], fl2_sem.at[b])
            wait_for(fr2.at[b], fr2_sem.at[b])
            g[i, core] = (hold[h, s] + fl2[b].astype(F32) + fr2[b].astype(F32)).astype(BF16)
            send(g.at[i, core], g.at[i, core], g_send.at[i], g_sem.at[i], partner).start()
            wait_for(w_old.at[i], w_sem.at[i])

            def take(m, v):
                w_new[i] = adamw(w_old[i].astype(F32), m, v, g[i, core].astype(F32))[0]

            @pl.when(i < wide)
            def _():
                wait_for(mv_own.at[i], mv_sem.at[i])
                wait_for(mv_par.at[i], mp_sem.at[i])

                def both(n):
                    mine, other = mv_own[i, n, :, core, :], mv_par[i, n, :, core, :]
                    return jnp.concatenate([jnp.where(core == 0, mine, other), jnp.where(core == 0, other, mine)], 0)

                take(both(0), both(1))

            @pl.when(i >= wide)
            def _():
                q = i - wide

                @pl.when(q // half == core)
                def _():
                    wait_for(mv_down.at[q], mv_sem.at[i])

                @pl.when(q // half != core)
                def _():
                    wait_for(mv_down.at[q], mp_sem.at[i])

                take(mv_down[q, 0], mv_down[q, 1])

            def share(part):
                send(w_new.at[i], part(f, 0, rows), n_send.at[i], nl_sem.at[i], right).start()
                send(w_new.at[i], part(f, 0, rows), f_send.at[i], nr_sem.at[i], left).start()
                pltpu.make_async_copy(w_new.at[i], part(f, 0, rows), n_own.at[i]).start()

            unit(i, share)

        @pl.when(t >= 5)
        def _():
            i = t - 5

            @pl.when(i < pieces)
            def _():
                wait_for(w_new.at[i], nl_sem.at[i])
                wait_for(w_new.at[i], nr_sem.at[i])
                wait_for(w_new.at[i], n_send.at[i])
                wait_for(w_new.at[i], f_send.at[i])

                def forward(part):
                    low, high = part(fm, 0, top), part(fp, top, rows - top)
                    send(low, low, n_send.at[i], no_sem.at[i], right).start()
                    send(high, high, f_send.at[i], no_sem.at[i], left).start()

                unit(i, forward)

    @pl.loop(0, pieces)
    def _(i):
        wait_for(g.at[i, core], g_sem.at[i])
        pltpu.make_async_copy(g.at[i], out.at[i], out_sem.at[i]).start()

    for n in range(SLOTS):
        slot = (pieces + n) % SLOTS
        wait_for(own.at[slot, pl.ds(0, last)], a_send.at[slot])
        wait_for(own.at[slot], par_send.at[slot])
    for n in range(HOLD):
        wait_for(sums.at[n, pl.ds(0, last)], s_send.at[n])

    @pl.loop(0, pieces)
    def _(i):
        wait_for(g.at[i, core], g_send.at[i])
        wait_for(w_new.at[i], n_own.at[i])
        wait_for(w_new.at[i], no_sem.at[i])
        wait_for(w_new.at[i, pl.ds(0, top)], n_send.at[i])
        wait_for(w_new.at[i, pl.ds(top, rows - top)], f_send.at[i])

        @pl.when(i < wide)
        def _():
            wait_for(mv_par.at[i], mp_send.at[i])

        @pl.when((i >= wide) & ((i - wide) // half == core))
        def _():
            wait_for(mv_down.at[0], mp_send.at[i])

        pltpu.make_async_copy(g.at[i], out.at[i], out_sem.at[i]).wait()


def reduce_and_step(terms, weights, m, v, side):
    _, layers, d, ff = terms[0].shape
    quarters = ff // d
    rows, cols = d // (side * side), d
    pieces, wide = 3 * quarters, 2 * quarters
    if side != 4 or layers != 2 or quarters != 4:
        raise ValueError("wrong sizes")
    top = (rows // 2 + 7) // 8 * 8
    dma = pltpu.SemaphoreType.DMA
    any_ = pl.BlockSpec(memory_space=pl.ANY)
    own = m[0].shape[0]
    one = functools.partial(jax.ShapeDtypeStruct, dtype=BF16)
    return pl.pallas_call(
        functools.partial(reduce_kernel, side, quarters, rows, cols),
        out_shape=[
            one((pieces, layers, rows, cols)),
            one((side, rows, ff)),
            one((side, rows, ff)),
            one((side, rows * quarters // 2, d)),
            one((side, rows * quarters // 2, d)),
        ],
        in_specs=[any_] * 12,
        out_specs=[any_] * 5,
        scratch_shapes=[
            pltpu.VMEM((SLOTS, side, side, rows, cols), BF16),
            pltpu.VMEM((SLOTS, side, side, rows, cols), BF16),
            pltpu.VMEM((RING_A, side // 2, rows, cols), BF16),
            pltpu.VMEM((RING_A, side // 2, rows, cols), BF16),
            pltpu.VMEM((RING_F, side, rows, cols), BF16),
            pltpu.VMEM((RING_F, side, rows, cols), BF16),
            pltpu.VMEM((HOLD, side, rows, cols), F32),
            pltpu.VMEM((HOLD, side, rows, cols), BF16),
            pltpu.VMEM((RING_A, top, cols), BF16),
            pltpu.VMEM((RING_A, rows - top, cols), BF16),
            pltpu.VMEM((RING_F, rows, cols), BF16),
            pltpu.VMEM((RING_F, rows, cols), BF16),
            pltpu.VMEM((pieces, layers, rows, cols), BF16),
            pltpu.VMEM((wide, 2, own, layers, cols), F32),
            pltpu.VMEM((wide, 2, own, layers, cols), F32),
            pltpu.VMEM((quarters, 2, rows, cols), F32),
            pltpu.VMEM((pieces, rows, cols), BF16),
            pltpu.VMEM((pieces, rows, cols), BF16),
            *(dma((SLOTS,)) for _ in range(4)),
            *(dma((RING_A,)) for _ in range(2)),
            *(dma((RING_F,)) for _ in range(2)),
            dma((HOLD,)),
            *(dma((RING_A,)) for _ in range(2)),
            *(dma((RING_F,)) for _ in range(2)),
            *(dma((pieces,)) for _ in range(3)),
            *(dma((pieces,)) for _ in range(10)),
            pltpu.SemaphoreType.REGULAR,
        ],
        compiler_params=pltpu.CompilerParams(collective_id=0, has_side_effects=True, vmem_limit_bytes=67043328),
        name="reduce_and_step",
    )(*terms, *weights, *m, *v)


def moments_kernel(side, quarters, rows, cols, *refs):
    pieces_ref, ins, outs = refs[0], refs[1:7], refs[7:13]
    g, bufs, g_sem, in_sem, out_sem = refs[13], refs[14:20], *refs[20:]
    core = Place(side).core
    half = quarters // 2
    g_load = pltpu.make_async_copy(pieces_ref, g, g_sem)
    g_load.start()
    loads = [pltpu.make_async_copy(ref, buf, in_sem.at[n]) for n, (ref, buf) in enumerate(zip(ins, bufs, strict=True))]
    stores = [pltpu.make_async_copy(buf, ref, out_sem.at[n]) for n, (ref, buf) in enumerate(zip(outs, bufs, strict=True))]
    for one in loads:
        one.start()
    g_load.wait()
    for n in range(3):
        m, v = bufs[n], bufs[3 + n]
        loads[n].wait()
        loads[3 + n].wait()

        if n < 2:

            @pl.loop(0, quarters)
            def _(q, n=n, m=m, v=v):
                at = pl.ds(pl.multiple_of(q * cols, 128), cols)
                for layer in range(2):
                    whole = g[n * quarters + q, layer].astype(F32)
                    grad = jnp.where(core == 0, whole[: rows // 2], whole[rows // 2 :])
                    m[:, layer, at] = 0.9 * m[:, layer, at] + 0.1 * grad
                    v[:, layer, at] = 0.95 * v[:, layer, at] + 0.05 * grad * grad

        else:

            @pl.loop(0, half)
            def _(q, n=n, m=m, v=v):
                at = pl.ds(pl.multiple_of(q * rows, 8), rows)
                for layer in range(2):
                    grad = g[n * quarters + core * half + q, layer].astype(F32)
                    m[layer, at] = 0.9 * m[layer, at] + 0.1 * grad
                    v[layer, at] = 0.95 * v[layer, at] + 0.05 * grad * grad

        stores[n].start()
        stores[3 + n].start()
    for one in stores:
        one.wait()


def moments(pieces, m, v, side, quarters):
    arrays = [*m, *v]
    any_ = pl.BlockSpec(memory_space=pl.ANY)
    rows, cols = pieces.shape[2:]
    size = sum(one.size for one in arrays)
    dma = pltpu.SemaphoreType.DMA
    return pl.pallas_call(
        functools.partial(moments_kernel, side, quarters, rows, cols),
        out_shape=[jax.ShapeDtypeStruct(one.shape, F32) for one in arrays],
        in_specs=[any_] * 7,
        out_specs=[any_] * 6,
        scratch_shapes=[
            pltpu.VMEM(pieces.shape, BF16),
            *(pltpu.VMEM(one.shape, F32) for one in arrays),
            dma,
            dma((6,)),
            dma((6,)),
        ],
        cost_estimate=pl.CostEstimate(flops=16 * size, bytes_accessed=8 * size, transcendentals=0),
        compiler_params=pltpu.CompilerParams(vmem_limit_bytes=67043328),
        name="moments",
    )(pieces, *arrays)


def place_kernel(side, jobs, n_in, has_out, *refs):
    ins = refs[:n_in]
    out = refs[n_in + has_out]
    scratch = refs[n_in + has_out + 1 :]
    bufs, in_sem, out_sem = scratch[:n_in], scratch[n_in], scratch[n_in + 1]
    at = Place(side)
    loads = [pltpu.make_async_copy(ref, buf, in_sem.at[n]) for n, (ref, buf) in enumerate(zip(ins, bufs, strict=True))]
    for one in loads:
        one.start()
    stores = []
    for n, (partner, along, first, per_chip) in enumerate(jobs):
        loads[n].wait()
        for bf in range(side):
            if partner:
                chip, layer = bf * at.ms + (at.f + along) % side * at.mf, 1 - at.core
            else:
                chip, layer = bf * at.mf + (at.s + along) % side * at.ms, at.core
            start = pl.multiple_of(chip * per_chip + first, 8)
            stores.append(pltpu.make_async_copy(bufs[n].at[bf], out.at[layer, pl.ds(start, bufs[n].shape[1])], out_sem.at[n, bf]))
            stores[-1].start()
    for one in stores:
        one.wait()


def place(side, shape, out, jobs):
    ins = [job[0] for job in jobs]
    size = sum(one.size for one in ins)
    any_ = pl.BlockSpec(memory_space=pl.ANY)
    has_out = out is not None
    return pl.pallas_call(
        functools.partial(place_kernel, side, [job[1:] for job in jobs], len(ins), has_out),
        out_shape=jax.ShapeDtypeStruct(shape, BF16),
        in_specs=[any_] * (len(ins) + has_out),
        out_specs=any_,
        input_output_aliases={len(ins): 0} if has_out else {},
        scratch_shapes=[pltpu.VMEM(one.shape, BF16) for one in ins]
        + [pltpu.SemaphoreType.DMA((len(ins),)), pltpu.SemaphoreType.DMA((len(ins), side))],
        cost_estimate=pl.CostEstimate(flops=4 * size, bytes_accessed=4 * size, transcendentals=0),
        compiler_params=pltpu.CompilerParams(vmem_limit_bytes=67043328),
        name="place",
    )(*ins, *((out,) if has_out else ()))


def solution(mesh):
    dp = mesh.shape["dp"]
    side = math.isqrt(dp // 2)

    def along(step):
        pairs = []
        for n in range(dp):
            core, x, y = n % 2, n // 2 // side, n // 2 % side
            x, y = (x, (y + step) % side) if core == 0 else ((x + step) % side, y)
            pairs.append((n, (x * side + y) * 2 + core))
        return pairs

    up, down = along(1), along(side - 1)
    swap = [(n, n + 1 - 2 * (n % 2)) for n in range(dp)]

    def move(x, pairs):
        return lax.ppermute(x, "dp", pairs)

    def step(*arrays):
        terms, weights, m, v = (arrays[i : i + 3] for i in (0, 3, 6, 9))
        quarters = terms[0].shape[3] // terms[0].shape[2]
        m, v = ([one.transpose(1, 0, 2) if n < 2 else one for n, one in enumerate(which)] for which in (m, v))
        pieces, *units = reduce_and_step(terms, weights, m, v, side)

        below = [move(x, up) for x in units]
        above = [move(x, down) for x in units]
        across = [move((below, above)[n % 2][n], (up, down)[n % 2]) for n in range(4)]
        stages = [[(0, x) for x in units], [(side - 1, x) for x in below], [(1, x) for x in above], [(2, x) for x in across]]
        per_chip = [weights[n].shape[1] // (side * side) for n in range(3)]

        whole = []
        for n in range(3):
            out = None
            for group in ((0,), (1, 2), (3,)):
                jobs = []
                for stage in group:
                    for part in (n,) if n < 2 else (2, 3):
                        steps, x = stages[stage][part]
                        first = x.shape[1] * (part - 2) if n == 2 else 0
                        jobs.append((x, False, steps, first, per_chip[n]))
                        jobs.append((move(x, swap), True, steps, first, per_chip[n]))
                out = place(side, weights[n].shape, out, jobs)
            whole.append(out)

        new = moments(pieces, m, v, side, quarters)
        return (*whole, *(one.transpose(1, 0, 2) if n % 3 < 2 else one for n, one in enumerate(new)))

    all_of, cut = P(None, None, None), P(None, "dp", None)
    return jax.shard_map(
        step,
        mesh=mesh,
        in_specs=(P(("rep", "dp"), None, None, None),) * 3 + (all_of,) * 3 + (cut,) * 6,
        out_specs=(P("rep", None, None),) * 3 + (P("rep", "dp", None),) * 6,
        check_vma=False,
    )
```

time: 468 us -> 422 us (0.902)
  Pallas kernels: 183 us -> 275 us
  waiting for transfers between devices: 193 us -> 116 us
  local copies, waits for them, and re-layouts: 68 us -> 1.23 us
  starting transfers between devices: 0.37 us -> 28.1 us
  between operations: 13.8 us -> 0.89 us
  other arithmetic: 9.97 us -> 0 us
    all_gather x3 -> x0, waiting for transfers between devices: 193 us -> none  [step(): whole = [lax.all_gather(one[0], 'dp', axis=1, tiled=True) for one in new]]
    ppermute x0 -> x28, waiting for transfers between devices: none -> 116 us  [move(): return lax.ppermute(x, 'dp', pairs)]
    pallas_call x1 -> x11, Pallas kernels: 183 us -> 275 us  [the longest x1 214 us: reduce_and_step(): pl.pallas_call(functools.partial(reduce_kernel, side, quarters, rows, col...]
    unnamed x11 -> x36, local copies, waits for them, and re-layouts: 58.2 us -> 1.23 us
    ppermute x0 -> x28, starting transfers between devices: none -> 28.1 us  [move(): return lax.ppermute(x, 'dp', pairs)]
    convert_element_type x2 -> x0, other arithmetic: 9.97 us -> none  [adamw(): return ((w - 0.02 * step).astype(BF16), m, v)]
  transfers between devices with their start and end apart: 3 -> 28, of which waited for: 3 -> 10; matrix products, arithmetic and copies ran while one was open for 9% -> 0% of each run, Pallas kernels for 0% -> 13%
where the time goes in v2:
time: 422 us
  Pallas kernels  275 us (65%)
  waiting for transfers between devices  116 us (27%)
  starting transfers between devices  28.1 us (7%)
    pallas_call x1, Pallas kernels, reduce_and_step(): pl.pallas_call(functools.partial(reduce_kernel, side, quarters, rows, col...  214 us
    ppermute x28, waiting for transfers between devices, move(): return lax.ppermute(x, 'dp', pairs)  116 us
    pallas_call x9, Pallas kernels, place(): pl.pallas_call(functools.partial(place_kernel, side, [job[1:] for job in...  50.4 us
    ppermute x28, starting transfers between devices, move(): return lax.ppermute(x, 'dp', pairs)  28.1 us
    pallas_call x1, Pallas kernels, moments(): pl.pallas_call(functools.partial(moments_kernel, side, quarters, rows, co...  10 us
  transfers between devices with their start and end apart: 28, of which 10 were waited for; matrix products, arithmetic and copies ran while one was open for 0% of the time, Pallas kernels for 13%

profile of v2, /device:TPU:97, one launch (start us, length us, event | category | flops | bytes accessed | tf_op | source)
XLA Modules:
  0.0 421.6 jit_solution(2734335297593876390)
XLA Ops:
  0.6 214.4 %reduce_and_step.1 = (bf16[12,2,72,1152]{3,2,1,0:T(8,128)(2,1)}, bf16[4,72,4608]{2,1,0:T(8,128)(2,1)}, bf16[4,72,4608]{2,1,0:T(8,128)(2,1)}, bf16[4,144,1152]{2,1,0:T(8,128)(2,1)}, bf16[4,144,1152]{2,1,0:T(8,128)(2,1)}) custom-call(bf16[1,2,1152,4608]{3,2,1,0:T(8,128)(2,1)} %refs_0_.1, bf16[1,2,1152,4608]{3,2,1,0:T(8,128)(2,1)} %refs_1_.1, ...), custom_call_target="tpu_custom_call" | custom-call | tf_op jit(solution)/shard_map/reduce_and_step/pallas_call | solution.py:360
  215.0 2.4 collective-permute-start.26
  217.4 0.0 collective-permute-start.14
  217.4 2.7 collective-permute-start.17
  220.1 0.7 collective-permute-start.27
  220.7 0.0 collective-permute-start.21
  220.7 0.0 collective-permute-done.26.refs_1_
  220.7 2.7 collective-permute-start.23
  223.4 12.3 %collective-permute-done.14.refs_0_ = bf16[4,144,1152]{2,1,0:T(8,128)(2,1)S(1)} collective-permute-done((bf16[4,144,1152]{2,1,0:T(8,128)(2,1)}, bf16[4,144,1152]{2,1,0:T(8,128)(2,1)S(1)}, u32[]{:S(2)}, u32[]{:S(2)}) %collective-permute-start.14) | collective-permute-done | bytes 1327136 | tf_op jit(solution)/shard_map/ppermute | solution.py:532
  235.7 1.0 collective-permute-start.20
  236.7 0.0 collective-permute-done.17.refs_6_
  236.7 0.1 collective-permute-start.25
  236.8 0.0 collective-permute-done.27.refs_3_
  236.8 1.2 copy-done.13
  238.0 0.6 collective-permute-start.13
  238.6 11.3 %collective-permute-done.21.refs_2_ = bf16[4,144,1152]{2,1,0:T(8,128)(2,1)S(1)} collective-permute-done((bf16[4,144,1152]{2,1,0:T(8,128)(2,1)}, bf16[4,144,1152]{2,1,0:T(8,128)(2,1)S(1)}, u32[]{:S(2)}, u32[]{:S(2)}) %collective-permute-start.21) | collective-permute-done | bytes 1327136 | tf_op jit(solution)/shard_map/ppermute | solution.py:532
  250.0 1.0 collective-permute-start.22
  250.9 0.0 collective-permute-done.23.refs_4_
  250.9 0.1 collective-permute-start.24
  251.0 0.0 collective-permute-done.20.refs_1_
  251.0 0.0 collective-permute-start.15
  251.1 0.0 collective-permute-done.25.refs_7_
  251.1 2.6 collective-permute-start.18
  253.7 0.0 collective-permute-done.22.refs_3_
  253.8 0.4 collective-permute-start.7
  254.2 1.3 collective-permute-done.24.refs_5_
  255.5 0.0 collective-permute-start.10
  255.5 13.7 %collective-permute-done.15.refs_0_ = bf16[4,144,1152]{2,1,0:T(8,128)(2,1)S(1)} collective-permute-done((bf16[4,144,1152]{2,1,0:T(8,128)(2,1)S(1)}, bf16[4,144,1152]{2,1,0:T(8,128)(2,1)S(1)}, u32[]{:S(2)}, u32[]{:S(2)}) %collective-permute-start.15) | collective-permute-done | bytes 1327136 | tf_op jit(solution)/shard_map/ppermute | solution.py:532
  269.2 0.0 collective-permute-start
  269.2 0.0 collective-permute-done.18.refs_2_
  269.2 1.4 collective-permute-start.6
  270.6 0.0 collective-permute-done.13.refs_1_
  270.6 1.5 collective-permute-start.4
  272.1 24.9 %collective-permute-done.7.refs_2_ = bf16[4,72,4608]{2,1,0:T(8,128)(2,1)S(1)} collective-permute-done((bf16[4,72,4608]{2,1,0:T(8,128)(2,1)}, bf16[4,72,4608]{2,1,0:T(8,128)(2,1)S(1)}, u32[]{:S(2)}, u32[]{:S(2)}) %collective-permute-start.7) | collective-permute-done | bytes 2654240 | tf_op jit(solution)/shard_map/ppermute | solution.py:532
  297.0 1.5 collective-permute-start.12
  298.5 0.0 collective-permute-done.10.refs_0_
  298.5 0.0 copy-done
  298.6 3.4 collective-permute-start.8
  302.0 24.2 %collective-permute-done.refs_0_ = bf16[4,72,4608]{2,1,0:T(8,128)(2,1)} collective-permute-done((bf16[4,72,4608]{2,1,0:T(8,128)(2,1)}, bf16[4,72,4608]{2,1,0:T(8,128)(2,1)}, u32[]{:S(2)}, u32[]{:S(2)}) %collective-permute-start) | collective-permute-done | bytes 2654240 | tf_op jit(solution)/shard_map/ppermute | solution.py:532
  326.2 0.0 collective-permute-start.1
  326.2 0.0 collective-permute-done.6.refs_1_
  326.2 1.4 collective-permute-start.16
  327.5 0.0 collective-permute-done.4.refs_2_
  327.5 0.1 collective-permute-start.19
  327.7 2.5 collective-permute-done.16.refs_1_
  330.2 0.4 collective-permute-start.11
  330.6 1.5 collective-permute-done.19.refs_3_
  332.1 0.4 collective-permute-start.3
  332.5 0.0 collective-permute-done.12.refs_3_
  332.5 0.1 collective-permute-start.5
  332.6 21.1 %collective-permute-done.8.refs_0_ = bf16[4,72,4608]{2,1,0:T(8,128)(2,1)} collective-permute-done((bf16[4,72,4608]{2,1,0:T(8,128)(2,1)S(1)}, bf16[4,72,4608]{2,1,0:T(8,128)(2,1)}, u32[]{:S(2)}, u32[]{:S(2)}) %collective-permute-start.8) | collective-permute-done | bytes 2654240 | tf_op jit(solution)/shard_map/ppermute | solution.py:532
  353.8 1.5 collective-permute-start.9
  355.3 3.5 collective-permute-done.1.refs_0_
  358.8 2.1 collective-permute-start.2
  361.0 10.0 %moments.1 = (f32[36,2,4608]{2,1,0:T(2,128)}, f32[36,2,4608]{2,1,0:T(2,128)}, f32[2,144,1152]{2,1,0:T(8,128)}, f32[36,2,4608]{2,1,0:T(2,128)}, f32[36,2,4608]{2,1,0:T(2,128)}, /*index=5*/f32[2,144,1152]{2,1,0:T(8,128)}) custom-call(bf16[12,2,72,1152]{3,2,1,0:T(8,128)(2,1)} %get-tuple-element.24.refs_0_, f32[36,2,4608]{2,1,0:T(2,128)} %bitcast.9, ...), custom_call_target="tpu_custom_call" | custom-call | flops 31850496 | bytes 15925248 | tf_op jit(solution)/shard_map/moments/pallas_call | solution.py:455
  371.0 4.4 %place.15.refs_8_ = bf16[2,4608,1152]{2,1,0:T(8,128)(2,1)} custom-call(bf16[4,144,1152]{2,1,0:T(8,128)(2,1)} %get-tuple-element.22.refs_0_, bf16[4,144,1152]{2,1,0:T(8,128)(2,1)} %copy-done.12, bf16[4,144,1152]{2,1,0:T(8,128)(2,1)} %get-tuple-element.23.refs_2_, bf16[4,144,1152]{2,1,0:T(8,128)(2,1)} %copy-done.13), custom_call_target="tpu_custom_call" | custom-call | flops 10616832 | bytes 10616832 | tf_op jit(solution)/shard_map/place/pallas_call | solution.py:502
  375.4 4.2 place.12.refs_4_
  379.6 4.2 place.9.refs_4_
  383.8 8.5 %place.16.refs_4_ = bf16[2,4608,1152]{2,1,0:T(8,128)(2,1)} custom-call(bf16[4,144,1152]{2,1,0:T(8,128)(2,1)} %copy-done.4, bf16[4,144,1152]{2,1,0:T(8,128)(2,1)} %copy-done.8, bf16[4,144,1152]{2,1,0:T(8,128)(2,1)} %copy-done.6, bf16[4,144,1152]{2,1,0:T(8,128)(2,1)} %copy-done.10, bf16[4,144,1152]{2,1,0:T(8,128)(2,1)} %copy-done.7, ...), custom_call_target="tpu_custom_call", output_to_operand_aliasing={{}: (8, {})} | custom-call | flops 21233664 | bytes 21233664 | tf_op jit(solution)/shard_map/place/pallas_call | solution.py:502
  392.3 4.4 %place.17 = bf16[2,4608,1152]{2,1,0:T(8,128)(2,1)} custom-call(bf16[4,144,1152]{2,1,0:T(8,128)(2,1)} %copy-done.14, bf16[4,144,1152]{2,1,0:T(8,128)(2,1)} %copy-done.16, bf16[4,144,1152]{2,1,0:T(8,128)(2,1)} %copy-done.15, bf16[4,144,1152]{2,1,0:T(8,128)(2,1)} %copy-done.17, bf16[2,4608,1152]{2,1,0:T(8,128)(2,1)} %place.16.refs_4_), custom_call_target="tpu_custom_call", output_to_operand_aliasing={{}: (4, {})} | custom-call | flops 10616832 | bytes 10616832 | tf_op jit(solution)/shard_map/place/pallas_call | solution.py:502
  396.7 8.2 %place.13.refs_2_ = bf16[2,1152,4608]{2,1,0:T(8,128)(2,1)} custom-call(bf16[4,72,4608]{2,1,0:T(8,128)(2,1)} %collective-permute-done.10.refs_0_, bf16[4,72,4608]{2,1,0:T(8,128)(2,1)} %collective-permute-done.11.refs_1_, bf16[4,72,4608]{2,1,0:T(8,128)(2,1)} %copy-done, bf16[4,72,4608]{2,1,0:T(8,128)(2,1)} %copy-done.1, ...), custom_call_target="tpu_custom_call", output_to_operand_aliasing={{}: (4, {})} | custom-call | flops 21233664 | bytes 21233664 | tf_op jit(solution)/shard_map/place/pallas_call | solution.py:502
  405.0 8.2 %place.10.refs_2_ = bf16[2,1152,4608]{2,1,0:T(8,128)(2,1)} custom-call(bf16[4,72,4608]{2,1,0:T(8,128)(2,1)} %collective-permute-done.refs_0_, bf16[4,72,4608]{2,1,0:T(8,128)(2,1)} %collective-permute-done.3.refs_1_, bf16[4,72,4608]{2,1,0:T(8,128)(2,1)} %collective-permute-done.4.refs_2_, ...), custom_call_target="tpu_custom_call", output_to_operand_aliasing={{}: (4, {})} | custom-call | flops 21233664 | bytes 21233664 | tf_op jit(solution)/shard_map/place/pallas_call | solution.py:502
  413.2 4.2 place.14
  417.4 4.2 place.11
  (39 shorter events, 0.1 us)
Async XLA Ops:
  215.0 5.7 %collective-permute-start.26 = (bf16[4,144,1152]{2,1,0:T(8,128)(2,1)}, bf16[4,144,1152]{2,1,0:T(8,128)(2,1)S(1)}, u32[]{:S(2)}, u32[]{:S(2)}) collective-permute-start(bf16[4,144,1152]{2,1,0:T(8,128)(2,1)} %get-tuple-element.22.refs_0_), channel_id=1, source_target_pairs={{0,1},{1,0},{2,3},{3,2},{4,5},{5,4},{6,7},{7,6},{8,9},{9,8},{10,11... | collective-permute-start | bytes 3981320 | tf_op jit(solution)/shard_map/ppermute | solution.py:532
  217.4 18.3 %collective-permute-start.14 = (bf16[4,144,1152]{2,1,0:T(8,128)(2,1)}, bf16[4,144,1152]{2,1,0:T(8,128)(2,1)S(1)}, u32[]{:S(2)}, u32[]{:S(2)}) collective-permute-start(bf16[4,144,1152]{2,1,0:T(8,128)(2,1)} %get-tuple-element.22.refs_0_), channel_id=1, source_target_pairs={{0,2},{1,9},{2,4},{3,11},{4,6},{5,13},{6,0},{7,15},{8,10},{9,17},{... | collective-permute-start | bytes 3981320 | tf_op jit(solution)/shard_map/ppermute | solution.py:532
  217.4 19.3 %collective-permute-start.17 = (bf16[4,144,1152]{2,1,0:T(8,128)(2,1)}, bf16[4,144,1152]{2,1,0:T(8,128)(2,1)S(1)}, u32[]{:S(2)}, u32[]{:S(2)}) collective-permute-start(bf16[4,144,1152]{2,1,0:T(8,128)(2,1)} %get-tuple-element.23.refs_2_), channel_id=1, source_target_pairs={{0,6},{1,25},{2,0},{3,27},{4,2},{5,29},{6,4},{7,31},{8,14},{9,1},{... | collective-permute-start | bytes 3981320 | tf_op jit(solution)/shard_map/ppermute | solution.py:532
  220.1 16.8 %collective-permute-start.27 = (bf16[4,144,1152]{2,1,0:T(8,128)(2,1)}, bf16[4,144,1152]{2,1,0:T(8,128)(2,1)S(1)}, u32[]{:S(2)}, u32[]{:S(2)}) collective-permute-start(bf16[4,144,1152]{2,1,0:T(8,128)(2,1)} %get-tuple-element.23.refs_2_), channel_id=1, source_target_pairs={{0,1},{1,0},{2,3},{3,2},{4,5},{5,4},{6,7},{7,6},{8,9},{9,8},{10,11... | collective-permute-start | bytes 3981320 | tf_op jit(solution)/shard_map/ppermute | solution.py:532
  220.7 29.2 %collective-permute-start.21 = (bf16[4,144,1152]{2,1,0:T(8,128)(2,1)}, bf16[4,144,1152]{2,1,0:T(8,128)(2,1)S(1)}, u32[]{:S(2)}, u32[]{:S(2)}) collective-permute-start(bf16[4,144,1152]{2,1,0:T(8,128)(2,1)} %get-tuple-element.23.refs_2_), channel_id=1, source_target_pairs={{0,2},{1,9},{2,4},{3,11},{4,6},{5,13},{6,0},{7,15},{8,10},{9,17},{... | collective-permute-start | bytes 3981320 | tf_op jit(solution)/shard_map/ppermute | solution.py:532
  220.7 2.7 copy-start.12
  220.7 30.2 %collective-permute-start.23 = (bf16[4,144,1152]{2,1,0:T(8,128)(2,1)}, bf16[4,144,1152]{2,1,0:T(8,128)(2,1)S(1)}, u32[]{:S(2)}, u32[]{:S(2)}) collective-permute-start(bf16[4,144,1152]{2,1,0:T(8,128)(2,1)} %get-tuple-element.22.refs_0_), channel_id=1, source_target_pairs={{0,6},{1,25},{2,0},{3,27},{4,2},{5,29},{6,4},{7,31},{8,14},{9,1},{... | collective-permute-start | bytes 3981320 | tf_op jit(solution)/shard_map/ppermute | solution.py:532
  235.7 33.5 %copy-start.4 = (bf16[4,144,1152]{2,1,0:T(8,128)(2,1)}, bf16[4,144,1152]{2,1,0:T(8,128)(2,1)S(1)}, u32[]{:S(2)}) copy-start(bf16[4,144,1152]{2,1,0:T(8,128)(2,1)S(1)} %collective-permute-done.14.refs_0_) | copy-start | bytes 3981316
  235.7 15.3 %collective-permute-start.20 = (bf16[4,144,1152]{2,1,0:T(8,128)(2,1)S(1)}, bf16[4,144,1152]{2,1,0:T(8,128)(2,1)S(1)}, u32[]{:S(2)}, u32[]{:S(2)}) collective-permute-start(bf16[4,144,1152]{2,1,0:T(8,128)(2,1)S(1)} %collective-permute-done.14.refs_0_), channel_id=1, source_target_pairs={{0,1},{1,0},{2,3},{3,2},{4,5},{5,4},{6,7},{7,6},{8,9},{9,8},{10,11... | collective-permute-start | bytes 3981320 | tf_op jit(solution)/shard_map/ppermute | solution.py:532
  236.7 32.5 %copy-start.5 = (bf16[4,144,1152]{2,1,0:T(8,128)(2,1)}, bf16[4,144,1152]{2,1,0:T(8,128)(2,1)S(1)}, u32[]{:S(2)}) copy-start(bf16[4,144,1152]{2,1,0:T(8,128)(2,1)S(1)} %collective-permute-done.17.refs_6_) | copy-start | bytes 3981316
  236.7 14.4 %collective-permute-start.25 = (bf16[4,144,1152]{2,1,0:T(8,128)(2,1)S(1)}, bf16[4,144,1152]{2,1,0:T(8,128)(2,1)S(1)}, u32[]{:S(2)}, u32[]{:S(2)}) collective-permute-start(bf16[4,144,1152]{2,1,0:T(8,128)(2,1)S(1)} %collective-permute-done.17.refs_6_), channel_id=1, source_target_pairs={{0,1},{1,0},{2,3},{3,2},{4,5},{5,4},{6,7},{7,6},{8,9},{9,8},{10,11... | collective-permute-start | bytes 3981320 | tf_op jit(solution)/shard_map/ppermute | solution.py:532
  236.8 1.2 copy-start.13
  238.0 32.6 %collective-permute-start.13 = (bf16[4,72,4608]{2,1,0:T(8,128)(2,1)}, bf16[4,72,4608]{2,1,0:T(8,128)(2,1)S(1)}, u32[]{:S(2)}, u32[]{:S(2)}) collective-permute-start(bf16[4,72,4608]{2,1,0:T(8,128)(2,1)} %get-tuple-element.21.refs_0_), channel_id=1, source_target_pairs={{0,1},{1,0},{2,3},{3,2},{4,5},{5,4},{6,7},{7,6},{8,9},{9,8},{10,11... | collective-permute-start | bytes 7962632 | tf_op jit(solution)/shard_map/ppermute | solution.py:532
  250.0 3.8 copy-start.6
  250.0 3.8 collective-permute-start.22
  250.9 107.9 %copy-start.7 = (bf16[4,144,1152]{2,1,0:T(8,128)(2,1)}, bf16[4,144,1152]{2,1,0:T(8,128)(2,1)S(1)}, u32[]{:S(2)}) copy-start(bf16[4,144,1152]{2,1,0:T(8,128)(2,1)S(1)} %collective-permute-done.23.refs_4_) | copy-start | bytes 3981316
  250.9 4.6 %collective-permute-start.24 = (bf16[4,144,1152]{2,1,0:T(8,128)(2,1)S(1)}, bf16[4,144,1152]{2,1,0:T(8,128)(2,1)S(1)}, u32[]{:S(2)}, u32[]{:S(2)}) collective-permute-start(bf16[4,144,1152]{2,1,0:T(8,128)(2,1)S(1)} %collective-permute-done.23.refs_4_), channel_id=1, source_target_pairs={{0,1},{1,0},{2,3},{3,2},{4,5},{5,4},{6,7},{7,6},{8,9},{9,8},{10,11... | collective-permute-start | bytes 3981320 | tf_op jit(solution)/shard_map/ppermute | solution.py:532
  251.0 2.7 copy-start.8
  251.0 18.1 %collective-permute-start.15 = (bf16[4,144,1152]{2,1,0:T(8,128)(2,1)S(1)}, bf16[4,144,1152]{2,1,0:T(8,128)(2,1)S(1)}, u32[]{:S(2)}, u32[]{:S(2)}) collective-permute-start(bf16[4,144,1152]{2,1,0:T(8,128)(2,1)S(1)} %collective-permute-done.14.refs_0_), channel_id=1, source_target_pairs={{0,2},{1,9},{2,4},{3,11},{4,6},{5,13},{6,0},{7,15},{8,10},{9,17},{... | collective-permute-start | bytes 3981320 | tf_op jit(solution)/shard_map/ppermute | solution.py:532
  251.1 109.9 %copy-start.9 = (bf16[4,144,1152]{2,1,0:T(8,128)(2,1)}, bf16[4,144,1152]{2,1,0:T(8,128)(2,1)S(1)}, u32[]{:S(2)}) copy-start(bf16[4,144,1152]{2,1,0:T(8,128)(2,1)S(1)} %collective-permute-done.25.refs_7_) | copy-start | bytes 3981316
  251.1 18.1 %collective-permute-start.18 = (bf16[4,144,1152]{2,1,0:T(8,128)(2,1)S(1)}, bf16[4,144,1152]{2,1,0:T(8,128)(2,1)S(1)}, u32[]{:S(2)}, u32[]{:S(2)}) collective-permute-start(bf16[4,144,1152]{2,1,0:T(8,128)(2,1)S(1)} %collective-permute-done.17.refs_6_), channel_id=1, source_target_pairs={{0,6},{1,25},{2,0},{3,27},{4,2},{5,29},{6,4},{7,31},{8,14},{9,1},{... | collective-permute-start | bytes 3981320 | tf_op jit(solution)/shard_map/ppermute | solution.py:532
  253.7 107.2 %copy-start.10 = (bf16[4,144,1152]{2,1,0:T(8,128)(2,1)}, bf16[4,144,1152]{2,1,0:T(8,128)(2,1)S(1)}, u32[]{:S(2)}) copy-start(bf16[4,144,1152]{2,1,0:T(8,128)(2,1)S(1)} %collective-permute-done.22.refs_3_) | copy-start | bytes 3981316
  253.8 43.3 %collective-permute-start.7 = (bf16[4,72,4608]{2,1,0:T(8,128)(2,1)}, bf16[4,72,4608]{2,1,0:T(8,128)(2,1)S(1)}, u32[]{:S(2)}, u32[]{:S(2)}) collective-permute-start(bf16[4,72,4608]{2,1,0:T(8,128)(2,1)} %get-tuple-element.21.refs_0_), channel_id=1, source_target_pairs={{0,6},{1,25},{2,0},{3,27},{4,2},{5,29},{6,4},{7,31},{8,14},{9,1},{... | collective-permute-start | bytes 7962632 | tf_op jit(solution)/shard_map/ppermute | solution.py:532
  255.5 105.5 %copy-start.11 = (bf16[4,144,1152]{2,1,0:T(8,128)(2,1)}, bf16[4,144,1152]{2,1,0:T(8,128)(2,1)S(1)}, u32[]{:S(2)}) copy-start(bf16[4,144,1152]{2,1,0:T(8,128)(2,1)S(1)} %collective-permute-done.24.refs_5_) | copy-start | bytes 3981316
  255.5 43.0 %collective-permute-start.10 = (bf16[4,72,4608]{2,1,0:T(8,128)(2,1)}, bf16[4,72,4608]{2,1,0:T(8,128)(2,1)}, u32[]{:S(2)}, u32[]{:S(2)}) collective-permute-start(bf16[4,72,4608]{2,1,0:T(8,128)(2,1)} %get-tuple-element.21.refs_0_), channel_id=1, source_target_pairs={{0,2},{1,9},{2,4},{3,11},{4,6},{5,13},{6,0},{7,15},{8,10},{9,17},{... | collective-permute-start | bytes 7962632 | tf_op jit(solution)/shard_map/ppermute | solution.py:532
  269.2 91.8 %copy-start.14 = (bf16[4,144,1152]{2,1,0:T(8,128)(2,1)}, bf16[4,144,1152]{2,1,0:T(8,128)(2,1)S(1)}, u32[]{:S(2)}) copy-start(bf16[4,144,1152]{2,1,0:T(8,128)(2,1)S(1)} %collective-permute-done.15.refs_0_) | copy-start | bytes 3981316
  269.2 57.0 %collective-permute-start = (bf16[4,72,4608]{2,1,0:T(8,128)(2,1)}, bf16[4,72,4608]{2,1,0:T(8,128)(2,1)}, u32[]{:S(2)}, u32[]{:S(2)}) collective-permute-start(bf16[4,72,4608]{2,1,0:T(8,128)(2,1)} %get-tuple-element.20.refs_0_), channel_id=1, source_target_pairs={{0,2},{1,9},{2,4},{3,11},{4,6},{5,13},{6,0},{7,15},{8,10},{9,17},{... | collective-permute-start | bytes 7962632 | tf_op jit(solution)/shard_map/ppermute | solution.py:532
  269.2 91.8 %copy-start.15 = (bf16[4,144,1152]{2,1,0:T(8,128)(2,1)}, bf16[4,144,1152]{2,1,0:T(8,128)(2,1)S(1)}, u32[]{:S(2)}) copy-start(bf16[4,144,1152]{2,1,0:T(8,128)(2,1)S(1)} %collective-permute-done.18.refs_2_) | copy-start | bytes 3981316
  269.2 56.9 %collective-permute-start.6 = (bf16[4,72,4608]{2,1,0:T(8,128)(2,1)}, bf16[4,72,4608]{2,1,0:T(8,128)(2,1)S(1)}, u32[]{:S(2)}, u32[]{:S(2)}) collective-permute-start(bf16[4,72,4608]{2,1,0:T(8,128)(2,1)} %get-tuple-element.20.refs_0_), channel_id=1, source_target_pairs={{0,1},{1,0},{2,3},{3,2},{4,5},{5,4},{6,7},{7,6},{8,9},{9,8},{10,11... | collective-permute-start | bytes 7962632 | tf_op jit(solution)/shard_map/ppermute | solution.py:532
  270.6 1.5 copy-start.2
  270.6 57.0 %collective-permute-start.4 = (bf16[4,72,4608]{2,1,0:T(8,128)(2,1)}, bf16[4,72,4608]{2,1,0:T(8,128)(2,1)}, u32[]{:S(2)}, u32[]{:S(2)}) collective-permute-start(bf16[4,72,4608]{2,1,0:T(8,128)(2,1)} %get-tuple-element.20.refs_0_), channel_id=1, source_target_pairs={{0,6},{1,25},{2,0},{3,27},{4,2},{5,29},{6,4},{7,31},{8,14},{9,1},{... | collective-permute-start | bytes 7962632 | tf_op jit(solution)/shard_map/ppermute | solution.py:532
  297.0 1.6 copy-start
  297.0 35.5 %collective-permute-start.12 = (bf16[4,72,4608]{2,1,0:T(8,128)(2,1)S(1)}, bf16[4,72,4608]{2,1,0:T(8,128)(2,1)S(1)}, u32[]{:S(2)}, u32[]{:S(2)}) collective-permute-start(bf16[4,72,4608]{2,1,0:T(8,128)(2,1)S(1)} %collective-permute-done.7.refs_2_), channel_id=1, source_target_pairs={{0,1},{1,0},{2,3},{3,2},{4,5},{5,4},{6,7},{7,6},{8,9},{9,8},{10,11... | collective-permute-start | bytes 7962632 | tf_op jit(solution)/shard_map/ppermute | solution.py:532
  298.6 55.2 %collective-permute-start.8 = (bf16[4,72,4608]{2,1,0:T(8,128)(2,1)S(1)}, bf16[4,72,4608]{2,1,0:T(8,128)(2,1)}, u32[]{:S(2)}, u32[]{:S(2)}) collective-permute-start(bf16[4,72,4608]{2,1,0:T(8,128)(2,1)S(1)} %collective-permute-done.7.refs_2_), channel_id=1, source_target_pairs={{0,6},{1,25},{2,0},{3,27},{4,2},{5,29},{6,4},{7,31},{8,14},{9,1},{... | collective-permute-start | bytes 7962632 | tf_op jit(solution)/shard_map/ppermute | solution.py:532
  326.2 32.7 %collective-permute-start.1 = (bf16[4,72,4608]{2,1,0:T(8,128)(2,1)}, bf16[4,72,4608]{2,1,0:T(8,128)(2,1)}, u32[]{:S(2)}, u32[]{:S(2)}) collective-permute-start(bf16[4,72,4608]{2,1,0:T(8,128)(2,1)} %collective-permute-done.refs_0_), channel_id=1, source_target_pairs={{0,2},{1,9},{2,4},{3,11},{4,6},{5,13},{6,0},{7,15},{8,10},{9,17},{... | collective-permute-start | bytes 7962632 | tf_op jit(solution)/shard_map/ppermute | solution.py:532
  326.2 29.1 %copy-start.3 = (bf16[4,72,4608]{2,1,0:T(8,128)(2,1)}, bf16[4,72,4608]{2,1,0:T(8,128)(2,1)S(1)}, u32[]{:S(2)}) copy-start(bf16[4,72,4608]{2,1,0:T(8,128)(2,1)S(1)} %collective-permute-done.6.refs_1_) | copy-start | bytes 7962628
  326.2 4.0 collective-permute-start.16
  327.5 4.6 %collective-permute-start.19 = (bf16[4,144,1152]{2,1,0:T(8,128)(2,1)S(1)}, bf16[4,144,1152]{2,1,0:T(8,128)(2,1)S(1)}, u32[]{:S(2)}, u32[]{:S(2)}) collective-permute-start(bf16[4,144,1152]{2,1,0:T(8,128)(2,1)S(1)} %collective-permute-done.18.refs_2_), channel_id=1, source_target_pairs={{0,1},{1,0},{2,3},{3,2},{4,5},{5,4},{6,7},{7,6},{8,9},{9,8},{10,11... | collective-permute-start | bytes 3981320 | tf_op jit(solution)/shard_map/ppermute | solution.py:532
  330.2 30.8 %copy-start.16 = (bf16[4,144,1152]{2,1,0:T(8,128)(2,1)}, bf16[4,144,1152]{2,1,0:T(8,128)(2,1)S(1)}, u32[]{:S(2)}) copy-start(bf16[4,144,1152]{2,1,0:T(8,128)(2,1)S(1)} %collective-permute-done.16.refs_1_) | copy-start | bytes 3981316
  330.2 66.5 %collective-permute-start.11 = (bf16[4,72,4608]{2,1,0:T(8,128)(2,1)}, bf16[4,72,4608]{2,1,0:T(8,128)(2,1)}, u32[]{:S(2)}, u32[]{:S(2)}) collective-permute-start(bf16[4,72,4608]{2,1,0:T(8,128)(2,1)} %collective-permute-done.10.refs_0_), channel_id=1, source_target_pairs={{0,1},{1,0},{2,3},{3,2},{4,5},{5,4},{6,7},{7,6},{8,9},{9,8},{10,11... | collective-permute-start | bytes 7962632 | tf_op jit(solution)/shard_map/ppermute | solution.py:532
  332.1 28.9 %copy-start.17 = (bf16[4,144,1152]{2,1,0:T(8,128)(2,1)}, bf16[4,144,1152]{2,1,0:T(8,128)(2,1)S(1)}, u32[]{:S(2)}) copy-start(bf16[4,144,1152]{2,1,0:T(8,128)(2,1)S(1)} %collective-permute-done.19.refs_3_) | copy-start | bytes 3981316
  332.1 72.8 %collective-permute-start.3 = (bf16[4,72,4608]{2,1,0:T(8,128)(2,1)}, bf16[4,72,4608]{2,1,0:T(8,128)(2,1)}, u32[]{:S(2)}, u32[]{:S(2)}) collective-permute-start(bf16[4,72,4608]{2,1,0:T(8,128)(2,1)} %collective-permute-done.refs_0_), channel_id=1, source_target_pairs={{0,1},{1,0},{2,3},{3,2},{4,5},{5,4},{6,7},{7,6},{8,9},{9,8},{10,11... | collective-permute-start | bytes 7962632 | tf_op jit(solution)/shard_map/ppermute | solution.py:532
  332.5 21.3 %copy-start.1 = (bf16[4,72,4608]{2,1,0:T(8,128)(2,1)}, bf16[4,72,4608]{2,1,0:T(8,128)(2,1)S(1)}, u32[]{:S(2)}) copy-start(bf16[4,72,4608]{2,1,0:T(8,128)(2,1)S(1)} %collective-permute-done.12.refs_3_) | copy-start | bytes 7962628
  332.5 72.4 %collective-permute-start.5 = (bf16[4,72,4608]{2,1,0:T(8,128)(2,1)}, bf16[4,72,4608]{2,1,0:T(8,128)(2,1)}, u32[]{:S(2)}, u32[]{:S(2)}) collective-permute-start(bf16[4,72,4608]{2,1,0:T(8,128)(2,1)} %collective-permute-done.4.refs_2_), channel_id=1, source_target_pairs={{0,1},{1,0},{2,3},{3,2},{4,5},{5,4},{6,7},{7,6},{8,9},{9,8},{10,11... | collective-permute-start | bytes 7962632 | tf_op jit(solution)/shard_map/ppermute | solution.py:532
  353.8 59.4 %collective-permute-start.9 = (bf16[4,72,4608]{2,1,0:T(8,128)(2,1)}, bf16[4,72,4608]{2,1,0:T(8,128)(2,1)}, u32[]{:S(2)}, u32[]{:S(2)}) collective-permute-start(bf16[4,72,4608]{2,1,0:T(8,128)(2,1)} %collective-permute-done.8.refs_0_), channel_id=1, source_target_pairs={{0,1},{1,0},{2,3},{3,2},{4,5},{5,4},{6,7},{7,6},{8,9},{9,8},{10,11... | collective-permute-start | bytes 7962632 | tf_op jit(solution)/shard_map/ppermute | solution.py:532
  358.8 58.5 %collective-permute-start.2 = (bf16[4,72,4608]{2,1,0:T(8,128)(2,1)}, bf16[4,72,4608]{2,1,0:T(8,128)(2,1)}, u32[]{:S(2)}, u32[]{:S(2)}) collective-permute-start(bf16[4,72,4608]{2,1,0:T(8,128)(2,1)} %collective-permute-done.1.refs_0_), channel_id=1, source_target_pairs={{0,1},{1,0},{2,3},{3,2},{4,5},{5,4},{6,7},{7,6},{8,9},{9,8},{10,11... | collective-permute-start | bytes 7962632 | tf_op jit(solution)/shard_map/ppermute | solution.py:532

commit v3 on v2

--- a/solution.py
+++ b/solution.py
@@ -14,6 +14,8 @@
 SLOTS = 4
 HOLD = 3
 RING_A, RING_F = 4, 6
+AHEAD = (2, 1, 3, 0)
+LATE = 4
 
 
 def adamw(w, m, v, g):
@@ -105,19 +107,21 @@
         slot = i % SLOTS
 
         def do(which, quarter):
-            @pl.loop(0, side * side)
-            def _(n):
-                bf, bs = n // side, n % side
-                send(
-                    block(terms, which, (0,), 1 - core, quarter, bf * at.ms + bs * at.mf),
-                    par.at[slot, bf, bs],
-                    par_send.at[slot],
-                    par_sem.at[slot],
-                    partner,
-                ).start()
-                pltpu.make_async_copy(
-                    block(terms, which, (0,), core, quarter, bf * at.mf + bs * at.ms), own.at[slot, bf, bs], own_sem.at[slot]
-                ).start()
+            for ahead in AHEAD:
+
+                @pl.loop(0, side)
+                def _(n, ahead=ahead):
+                    theirs, mine = (s + ahead) % side, (f + ahead) % side
+                    send(
+                        block(terms, which, (0,), 1 - core, quarter, theirs * at.ms + n * at.mf),
+                        par.at[slot, theirs, n],
+                        par_send.at[slot],
+                        par_sem.at[slot, ahead],
+                        partner,
+                    ).start()
+                    pltpu.make_async_copy(
+                        block(terms, which, (0,), core, quarter, mine * at.mf + n * at.ms), own.at[slot, mine, n], own_sem.at[slot, ahead]
+                    ).start()
 
         each(i, do)
 
@@ -156,6 +160,14 @@
     def pair(slot, bf, bs):
         return own[slot, bf, bs].astype(F32) + par[slot, bf, bs].astype(F32)
 
+    def arrive(slot, ahead):
+        wait_for(own.at[slot, 0], own_sem.at[slot, ahead])
+        wait_for(par.at[slot, 0], par_sem.at[slot, ahead])
+
+    def shared(t):
+        n = t - 3 - LATE + jnp.maximum(t + 1 - pieces, 0)
+        return jnp.clip(n, 0, jnp.minimum(jnp.maximum(t - 3, 0), pieces))
+
     load(0)
     load(1)
 
@@ -165,8 +177,7 @@
         def _():
             i, slot = t, t % SLOTS
             a, b = i % RING_A, i % RING_F
-            wait_for(own.at[slot], own_sem.at[slot])
-            wait_for(par.at[slot], par_sem.at[slot])
+            arrive(slot, 2)
 
             @pl.loop(0, side)
             def _(n):
@@ -174,6 +185,9 @@
 
             send(own.at[slot, f2, pl.ds(0, half)], ra.at[a], a_send.at[slot], ra_sem.at[a], right).start()
             send(own.at[slot, f2, pl.ds(half, half)], rb.at[a], a_send.at[slot], rb_sem.at[a], left).start()
+
+            arrive(slot, 1)
+            arrive(slot, last)
 
             @pl.loop(0, half)
             def _(n):
@@ -207,6 +221,7 @@
             def _():
                 wait_for(sums.at[h, pl.ds(0, last)], s_send.at[h])
 
+            arrive(slot, 0)
             wait_for(fl.at[b], fl_sem.at[b])
             wait_for(fr.at[b], fr_sem.at[b])
 
@@ -289,6 +304,8 @@
 
                 take(mv_down[q, 0], mv_down[q, 1])
 
+        @pl.loop(shared(t - 1), shared(t))
+        def _(i):
             def share(part):
                 send(w_new.at[i], part(f, 0, rows), n_send.at[i], nl_sem.at[i], right).start()
                 send(w_new.at[i], part(f, 0, rows), f_send.at[i], nr_sem.at[i], left).start()
@@ -296,23 +313,19 @@
 
             unit(i, share)
 
-        @pl.when(t >= 5)
-        def _():
-            i = t - 5
-
-            @pl.when(i < pieces)
-            def _():
-                wait_for(w_new.at[i], nl_sem.at[i])
-                wait_for(w_new.at[i], nr_sem.at[i])
-                wait_for(w_new.at[i], n_send.at[i])
-                wait_for(w_new.at[i], f_send.at[i])
-
-                def forward(part):
-                    low, high = part(fm, 0, top), part(fp, top, rows - top)
-                    send(low, low, n_send.at[i], no_sem.at[i], right).start()
-                    send(high, high, f_send.at[i], no_sem.at[i], left).start()
-
-                unit(i, forward)
+        @pl.loop(shared(t - 2), shared(t - 1))
+        def _(i):
+            wait_for(w_new.at[i], nl_sem.at[i])
+            wait_for(w_new.at[i], nr_sem.at[i])
+            wait_for(w_new.at[i], n_send.at[i])
+            wait_for(w_new.at[i], f_send.at[i])
+
+            def forward(part):
+                low, high = part(fm, 0, top), part(fp, top, rows - top)
+                send(low, low, n_send.at[i], no_sem.at[i], right).start()
+                send(high, high, f_send.at[i], no_sem.at[i], left).start()
+
+            unit(i, forward)
 
     @pl.loop(0, pieces)
     def _(i):
@@ -387,7 +400,10 @@
             pltpu.VMEM((quarters, 2, rows, cols), F32),
             pltpu.VMEM((pieces, rows, cols), BF16),
             pltpu.VMEM((pieces, rows, cols), BF16),
-            *(dma((SLOTS,)) for _ in range(4)),
+            dma((SLOTS, side)),
+            dma((SLOTS,)),
+            dma((SLOTS, side)),
+            dma((SLOTS,)),
             *(dma((RING_A,)) for _ in range(2)),
             *(dma((RING_F,)) for _ in range(2)),
             dma((HOLD,)),
@@ -546,15 +562,18 @@
         whole = []
         for n in range(3):
             out = None
-            for group in ((0,), (1, 2), (3,)):
-                jobs = []
+            for when, group in enumerate(((0,), (1, 2), (3,))):
+                here, there = [], []
                 for stage in group:
                     for part in (n,) if n < 2 else (2, 3):
                         steps, x = stages[stage][part]
                         first = x.shape[1] * (part - 2) if n == 2 else 0
-                        jobs.append((x, False, steps, first, per_chip[n]))
-                        jobs.append((move(x, swap), True, steps, first, per_chip[n]))
-                out = place(side, weights[n].shape, out, jobs)
+                        here.append((x, False, steps, first, per_chip[n]))
+                        there.append((move(x, swap), True, steps, first, per_chip[n]))
+                if (when, n) == (2, 2):
+                    out = place(side, weights[n].shape, out, here)
+                    here = []
+                out = place(side, weights[n].shape, out, here + there)
             whole.append(out)
 
         new = moments(pieces, m, v, side, quarters)

time: 422 us -> 416 us (0.986)
    pallas_call x1, Pallas kernels: 214 us -> 209 us  [reduce_and_step(): pl.pallas_call(functools.partial(reduce_kernel, side, quarters, rows, col...]
    pallas_call x9 -> x10, Pallas kernels: 50.4 us -> 51.9 us  [place(): pl.pallas_call(functools.partial(place_kernel, side, [job[1:] for job in...]
  transfers between devices with their start and end apart: 28 -> 28, of which waited for: 10 -> 10; matrix products, arithmetic and copies ran while one was open for 0% -> 0% of each run, Pallas kernels for 13% -> 14%
where the time goes in v3:
time: 416 us; the launch traced here: 415 us
  Pallas kernels  271 us (65%)
  waiting for transfers between devices  115 us (28%)
  starting transfers between devices  27.5 us (7%)
    pallas_call x1, Pallas kernels, reduce_and_step(): pl.pallas_call(functools.partial(reduce_kernel, side, quarters, rows, col...  209 us
    ppermute x28, waiting for transfers between devices, move(): return lax.ppermute(x, 'dp', pairs)  115 us
    pallas_call x10, Pallas kernels, place(): pl.pallas_call(functools.partial(place_kernel, side, [job[1:] for job in...  51.9 us
    ppermute x28, starting transfers between devices, move(): return lax.ppermute(x, 'dp', pairs)  27.5 us
    pallas_call x1, Pallas kernels, moments(): pl.pallas_call(functools.partial(moments_kernel, side, quarters, rows, co...  10 us
  transfers between devices with their start and end apart: 28, of which 10 were waited for; matrix products, arithmetic and copies ran while one was open for 0% of the time, Pallas kernels for 14%

profile of v3, /device:TPU:97, one launch (start us, length us, event | category | flops | bytes accessed | tf_op | source)
XLA Modules:
  0.0 415.5 jit_solution(9250616609309509725)
XLA Ops:
  0.6 208.7 %reduce_and_step.1 = (bf16[12,2,72,1152]{3,2,1,0:T(8,128)(2,1)}, bf16[4,72,4608]{2,1,0:T(8,128)(2,1)}, bf16[4,72,4608]{2,1,0:T(8,128)(2,1)}, bf16[4,144,1152]{2,1,0:T(8,128)(2,1)}, bf16[4,144,1152]{2,1,0:T(8,128)(2,1)}) custom-call(bf16[1,2,1152,4608]{3,2,1,0:T(8,128)(2,1)} %refs_0_.1, bf16[1,2,1152,4608]{3,2,1,0:T(8,128)(2,1)} %refs_1_.1, ...), custom_call_target="tpu_custom_call" | custom-call | tf_op jit(solution)/shard_map/reduce_and_step/pallas_call | solution.py:373
  209.3 0.5 collective-permute-start.26
  209.8 0.6 collective-permute-start.14
  210.5 2.0 collective-permute-start.17
  212.5 0.7 collective-permute-start.27
  213.2 0.6 collective-permute-start.20
  213.8 0.0 collective-permute-done.26.refs_2_
  213.8 2.0 collective-permute-start.21
  215.9 12.3 %collective-permute-done.14.refs_0_ = bf16[4,144,1152]{2,1,0:T(8,128)(2,1)S(1)} collective-permute-done((bf16[4,144,1152]{2,1,0:T(8,128)(2,1)}, bf16[4,144,1152]{2,1,0:T(8,128)(2,1)S(1)}, u32[]{:S(2)}, u32[]{:S(2)}) %collective-permute-start.14) | collective-permute-done | bytes 1327136 | tf_op jit(solution)/shard_map/ppermute | solution.py:548
  228.2 1.0 collective-permute-start.22
  229.2 0.0 collective-permute-done.17.refs_3_
  229.2 0.1 collective-permute-start.25
  229.3 0.0 collective-permute-done.27.refs_3_
  229.3 1.2 copy-done.13
  230.4 0.6 collective-permute-start.13
  231.1 11.3 %collective-permute-done.20.refs_1_ = bf16[4,144,1152]{2,1,0:T(8,128)(2,1)S(1)} collective-permute-done((bf16[4,144,1152]{2,1,0:T(8,128)(2,1)}, bf16[4,144,1152]{2,1,0:T(8,128)(2,1)S(1)}, u32[]{:S(2)}, u32[]{:S(2)}) %collective-permute-start.20) | collective-permute-done | bytes 1327136 | tf_op jit(solution)/shard_map/ppermute | solution.py:548
  242.4 1.0 collective-permute-start.23
  243.4 0.0 collective-permute-done.21.refs_2_
  243.4 0.1 collective-permute-start.24
  243.5 0.0 collective-permute-done.22.refs_4_
  243.5 0.6 collective-permute-start.15
  244.1 0.0 collective-permute-done.25.refs_7_
  244.1 2.0 collective-permute-start.18
  246.2 0.0 collective-permute-done.23.refs_5_
  246.2 1.5 collective-permute-start.7
  247.7 0.2 collective-permute-done.24.refs_6_
  248.0 0.6 collective-permute-start.10
  248.6 13.0 %collective-permute-done.15.refs_0_ = bf16[4,144,1152]{2,1,0:T(8,128)(2,1)S(1)} collective-permute-done((bf16[4,144,1152]{2,1,0:T(8,128)(2,1)S(1)}, bf16[4,144,1152]{2,1,0:T(8,128)(2,1)S(1)}, u32[]{:S(2)}, u32[]{:S(2)}) %collective-permute-start.15) | collective-permute-done | bytes 1327136 | tf_op jit(solution)/shard_map/ppermute | solution.py:548
  261.6 0.0 collective-permute-start
  261.7 0.0 collective-permute-done.18.refs_1_
  261.7 1.4 collective-permute-start.6
  263.0 0.0 collective-permute-done.13.refs_1_
  263.0 1.7 collective-permute-start.3
  264.7 24.9 %collective-permute-done.7.refs_1_ = bf16[4,72,4608]{2,1,0:T(8,128)(2,1)S(1)} collective-permute-done((bf16[4,72,4608]{2,1,0:T(8,128)(2,1)}, bf16[4,72,4608]{2,1,0:T(8,128)(2,1)S(1)}, u32[]{:S(2)}, u32[]{:S(2)}) %collective-permute-start.7) | collective-permute-done | bytes 2654240 | tf_op jit(solution)/shard_map/ppermute | solution.py:548
  289.6 1.4 collective-permute-start.12
  291.0 0.0 collective-permute-done.10.refs_0_
  291.0 0.2 copy-done
  291.2 3.2 collective-permute-start.8
  294.4 24.2 %collective-permute-done.refs_0_ = bf16[4,72,4608]{2,1,0:T(8,128)(2,1)} collective-permute-done((bf16[4,72,4608]{2,1,0:T(8,128)(2,1)}, bf16[4,72,4608]{2,1,0:T(8,128)(2,1)}, u32[]{:S(2)}, u32[]{:S(2)}) %collective-permute-start) | collective-permute-done | bytes 2654240 | tf_op jit(solution)/shard_map/ppermute | solution.py:548
  318.6 1.4 collective-permute-start.16
  320.0 0.0 collective-permute-done.3.refs_1_
  320.0 0.1 collective-permute-start.19
  320.1 2.5 collective-permute-done.16.refs_0_
  322.7 0.4 collective-permute-start.11
  323.0 1.5 collective-permute-done.19.refs_1_
  324.6 0.4 collective-permute-start.4
  325.0 0.1 collective-permute-start.5
  325.1 21.4 %collective-permute-done.8.refs_0_ = bf16[4,72,4608]{2,1,0:T(8,128)(2,1)} collective-permute-done((bf16[4,72,4608]{2,1,0:T(8,128)(2,1)S(1)}, bf16[4,72,4608]{2,1,0:T(8,128)(2,1)}, u32[]{:S(2)}, u32[]{:S(2)}) %collective-permute-start.8) | collective-permute-done | bytes 2654240 | tf_op jit(solution)/shard_map/ppermute | solution.py:548
  346.5 1.3 collective-permute-start.9
  347.8 3.5 collective-permute-done.1.refs_0_
  351.3 2.1 collective-permute-start.2
  353.5 10.0 %moments.1 = (f32[36,2,4608]{2,1,0:T(2,128)}, f32[36,2,4608]{2,1,0:T(2,128)}, f32[2,144,1152]{2,1,0:T(8,128)}, f32[36,2,4608]{2,1,0:T(2,128)}, f32[36,2,4608]{2,1,0:T(2,128)}, /*index=5*/f32[2,144,1152]{2,1,0:T(8,128)}) custom-call(bf16[12,2,72,1152]{3,2,1,0:T(8,128)(2,1)} %get-tuple-element.24.refs_0_, f32[36,2,4608]{2,1,0:T(2,128)} %bitcast.9, ...), custom_call_target="tpu_custom_call" | custom-call | flops 31850496 | bytes 15925248 | tf_op jit(solution)/shard_map/moments/pallas_call | solution.py:471
  363.5 4.4 %place.16.refs_8_ = bf16[2,4608,1152]{2,1,0:T(8,128)(2,1)} custom-call(bf16[4,144,1152]{2,1,0:T(8,128)(2,1)} %get-tuple-element.22.refs_0_, bf16[4,144,1152]{2,1,0:T(8,128)(2,1)} %get-tuple-element.23.refs_1_, bf16[4,144,1152]{2,1,0:T(8,128)(2,1)} %copy-done.12, bf16[4,144,1152]{2,1,0:T(8,128)(2,1)} %copy-done.13), custom_call_target="tpu_custom_call" | custom-call | flops 10616832 | bytes 10616832 | tf_op jit(solution)/shard_map/place/pallas_call | solution.py:518
  367.9 8.5 %place.17.refs_2_ = bf16[2,4608,1152]{2,1,0:T(8,128)(2,1)} custom-call(bf16[4,144,1152]{2,1,0:T(8,128)(2,1)} %copy-done.4, bf16[4,144,1152]{2,1,0:T(8,128)(2,1)} %copy-done.6, bf16[4,144,1152]{2,1,0:T(8,128)(2,1)} %copy-done.7, bf16[4,144,1152]{2,1,0:T(8,128)(2,1)} %copy-done.5, bf16[4,144,1152]{2,1,0:T(8,128)(2,1)} %copy-done.8, ...), custom_call_target="tpu_custom_call", output_to_operand_aliasing={{}: (8, {})} | custom-call | flops 21233664 | bytes 21233664 | tf_op jit(solution)/shard_map/place/pallas_call | solution.py:518
  376.4 2.9 place.18.refs_2_
  379.3 4.2 %place.13.refs_4_ = bf16[2,1152,4608]{2,1,0:T(8,128)(2,1)} custom-call(bf16[4,72,4608]{2,1,0:T(8,128)(2,1)} %get-tuple-element.21.refs_0_, bf16[4,72,4608]{2,1,0:T(8,128)(2,1)} %copy-done.2), custom_call_target="tpu_custom_call" | custom-call | flops 10616832 | bytes 10616832 | tf_op jit(solution)/shard_map/place/pallas_call | solution.py:518
  383.5 4.2 %place.10.refs_4_ = bf16[2,1152,4608]{2,1,0:T(8,128)(2,1)} custom-call(bf16[4,72,4608]{2,1,0:T(8,128)(2,1)} %get-tuple-element.20.refs_0_, bf16[4,72,4608]{2,1,0:T(8,128)(2,1)} %copy-done.3), custom_call_target="tpu_custom_call" | custom-call | flops 10616832 | bytes 10616832 | tf_op jit(solution)/shard_map/place/pallas_call | solution.py:518
  387.7 2.9 place.19
  390.6 8.2 %place.14.refs_2_ = bf16[2,1152,4608]{2,1,0:T(8,128)(2,1)} custom-call(bf16[4,72,4608]{2,1,0:T(8,128)(2,1)} %collective-permute-done.10.refs_0_, bf16[4,72,4608]{2,1,0:T(8,128)(2,1)} %copy-done, bf16[4,72,4608]{2,1,0:T(8,128)(2,1)} %collective-permute-done.11.refs_2_, bf16[4,72,4608]{2,1,0:T(8,128)(2,1)} %copy-done.1, ...), custom_call_target="tpu_custom_call", output_to_operand_aliasing={{}: (4, {})} | custom-call | flops 21233664 | bytes 21233664 | tf_op jit(solution)/shard_map/place/pallas_call | solution.py:518
  398.8 0.0 collective-permute-done.5.refs_3_
  398.8 8.2 %place.11.refs_2_ = bf16[2,1152,4608]{2,1,0:T(8,128)(2,1)} custom-call(bf16[4,72,4608]{2,1,0:T(8,128)(2,1)} %collective-permute-done.refs_0_, bf16[4,72,4608]{2,1,0:T(8,128)(2,1)} %collective-permute-done.3.refs_1_, bf16[4,72,4608]{2,1,0:T(8,128)(2,1)} %collective-permute-done.4.refs_2_, ...), custom_call_target="tpu_custom_call", output_to_operand_aliasing={{}: (4, {})} | custom-call | flops 21233664 | bytes 21233664 | tf_op jit(solution)/shard_map/place/pallas_call | solution.py:518
  407.0 0.0 collective-permute-done.9.refs_1_
  407.1 4.2 %place.15 = bf16[2,1152,4608]{2,1,0:T(8,128)(2,1)} custom-call(bf16[4,72,4608]{2,1,0:T(8,128)(2,1)} %collective-permute-done.8.refs_0_, bf16[4,72,4608]{2,1,0:T(8,128)(2,1)} %collective-permute-done.9.refs_1_, bf16[2,1152,4608]{2,1,0:T(8,128)(2,1)} %place.14.refs_2_), custom_call_target="tpu_custom_call", output_to_operand_aliasing={{}: (2, {})} | custom-call | flops 10616832 | bytes 10616832 | tf_op jit(solution)/shard_map/place/pallas_call | solution.py:518
  411.3 4.2 %place.12 = bf16[2,1152,4608]{2,1,0:T(8,128)(2,1)} custom-call(bf16[4,72,4608]{2,1,0:T(8,128)(2,1)} %collective-permute-done.1.refs_0_, bf16[4,72,4608]{2,1,0:T(8,128)(2,1)} %collective-permute-done.2.refs_1_, bf16[2,1152,4608]{2,1,0:T(8,128)(2,1)} %place.11.refs_2_), custom_call_target="tpu_custom_call", output_to_operand_aliasing={{}: (2, {})} | custom-call | flops 10616832 | bytes 10616832 | tf_op jit(solution)/shard_map/place/pallas_call | solution.py:518
  (40 shorter events, 0.1 us)
Async XLA Ops:
  209.3 4.5 %collective-permute-start.26 = (bf16[4,144,1152]{2,1,0:T(8,128)(2,1)}, bf16[4,144,1152]{2,1,0:T(8,128)(2,1)S(1)}, u32[]{:S(2)}, u32[]{:S(2)}) collective-permute-start(bf16[4,144,1152]{2,1,0:T(8,128)(2,1)} %get-tuple-element.22.refs_0_), channel_id=1, source_target_pairs={{0,1},{1,0},{2,3},{3,2},{4,5},{5,4},{6,7},{7,6},{8,9},{9,8},{10,11... | collective-permute-start | bytes 3981320 | tf_op jit(solution)/shard_map/ppermute | solution.py:548
  209.8 18.3 %collective-permute-start.14 = (bf16[4,144,1152]{2,1,0:T(8,128)(2,1)}, bf16[4,144,1152]{2,1,0:T(8,128)(2,1)S(1)}, u32[]{:S(2)}, u32[]{:S(2)}) collective-permute-start(bf16[4,144,1152]{2,1,0:T(8,128)(2,1)} %get-tuple-element.22.refs_0_), channel_id=1, source_target_pairs={{0,2},{1,9},{2,4},{3,11},{4,6},{5,13},{6,0},{7,15},{8,10},{9,17},{... | collective-permute-start | bytes 3981320 | tf_op jit(solution)/shard_map/ppermute | solution.py:548
  210.5 18.7 %collective-permute-start.17 = (bf16[4,144,1152]{2,1,0:T(8,128)(2,1)}, bf16[4,144,1152]{2,1,0:T(8,128)(2,1)S(1)}, u32[]{:S(2)}, u32[]{:S(2)}) collective-permute-start(bf16[4,144,1152]{2,1,0:T(8,128)(2,1)} %get-tuple-element.23.refs_1_), channel_id=1, source_target_pairs={{0,6},{1,25},{2,0},{3,27},{4,2},{5,29},{6,4},{7,31},{8,14},{9,1},{... | collective-permute-start | bytes 3981320 | tf_op jit(solution)/shard_map/ppermute | solution.py:548
  212.5 16.8 %collective-permute-start.27 = (bf16[4,144,1152]{2,1,0:T(8,128)(2,1)}, bf16[4,144,1152]{2,1,0:T(8,128)(2,1)S(1)}, u32[]{:S(2)}, u32[]{:S(2)}) collective-permute-start(bf16[4,144,1152]{2,1,0:T(8,128)(2,1)} %get-tuple-element.23.refs_1_), channel_id=1, source_target_pairs={{0,1},{1,0},{2,3},{3,2},{4,5},{5,4},{6,7},{7,6},{8,9},{9,8},{10,11... | collective-permute-start | bytes 3981320 | tf_op jit(solution)/shard_map/ppermute | solution.py:548
  213.2 29.2 %collective-permute-start.20 = (bf16[4,144,1152]{2,1,0:T(8,128)(2,1)}, bf16[4,144,1152]{2,1,0:T(8,128)(2,1)S(1)}, u32[]{:S(2)}, u32[]{:S(2)}) collective-permute-start(bf16[4,144,1152]{2,1,0:T(8,128)(2,1)} %get-tuple-element.23.refs_1_), channel_id=1, source_target_pairs={{0,2},{1,9},{2,4},{3,11},{4,6},{5,13},{6,0},{7,15},{8,10},{9,17},{... | collective-permute-start | bytes 3981320 | tf_op jit(solution)/shard_map/ppermute | solution.py:548
  213.8 2.0 copy-start.12
  213.8 29.5 %collective-permute-start.21 = (bf16[4,144,1152]{2,1,0:T(8,128)(2,1)}, bf16[4,144,1152]{2,1,0:T(8,128)(2,1)S(1)}, u32[]{:S(2)}, u32[]{:S(2)}) collective-permute-start(bf16[4,144,1152]{2,1,0:T(8,128)(2,1)} %get-tuple-element.22.refs_0_), channel_id=1, source_target_pairs={{0,6},{1,25},{2,0},{3,27},{4,2},{5,29},{6,4},{7,31},{8,14},{9,1},{... | collective-permute-start | bytes 3981320 | tf_op jit(solution)/shard_map/ppermute | solution.py:548
  228.2 33.5 %copy-start.4 = (bf16[4,144,1152]{2,1,0:T(8,128)(2,1)}, bf16[4,144,1152]{2,1,0:T(8,128)(2,1)S(1)}, u32[]{:S(2)}) copy-start(bf16[4,144,1152]{2,1,0:T(8,128)(2,1)S(1)} %collective-permute-done.14.refs_0_) | copy-start | bytes 3981316
  228.2 15.3 %collective-permute-start.22 = (bf16[4,144,1152]{2,1,0:T(8,128)(2,1)S(1)}, bf16[4,144,1152]{2,1,0:T(8,128)(2,1)S(1)}, u32[]{:S(2)}, u32[]{:S(2)}) collective-permute-start(bf16[4,144,1152]{2,1,0:T(8,128)(2,1)S(1)} %collective-permute-done.14.refs_0_), channel_id=1, source_target_pairs={{0,1},{1,0},{2,3},{3,2},{4,5},{5,4},{6,7},{7,6},{8,9},{9,8},{10,11... | collective-permute-start | bytes 3981320 | tf_op jit(solution)/shard_map/ppermute | solution.py:548
  229.2 32.5 %copy-start.5 = (bf16[4,144,1152]{2,1,0:T(8,128)(2,1)}, bf16[4,144,1152]{2,1,0:T(8,128)(2,1)S(1)}, u32[]{:S(2)}) copy-start(bf16[4,144,1152]{2,1,0:T(8,128)(2,1)S(1)} %collective-permute-done.17.refs_3_) | copy-start | bytes 3981316
  229.2 15.0 %collective-permute-start.25 = (bf16[4,144,1152]{2,1,0:T(8,128)(2,1)S(1)}, bf16[4,144,1152]{2,1,0:T(8,128)(2,1)S(1)}, u32[]{:S(2)}, u32[]{:S(2)}) collective-permute-start(bf16[4,144,1152]{2,1,0:T(8,128)(2,1)S(1)} %collective-permute-done.17.refs_3_), channel_id=1, source_target_pairs={{0,1},{1,0},{2,3},{3,2},{4,5},{5,4},{6,7},{7,6},{8,9},{9,8},{10,11... | collective-permute-start | bytes 3981320 | tf_op jit(solution)/shard_map/ppermute | solution.py:548
  229.3 1.2 copy-start.13
  230.4 32.6 %collective-permute-start.13 = (bf16[4,72,4608]{2,1,0:T(8,128)(2,1)}, bf16[4,72,4608]{2,1,0:T(8,128)(2,1)S(1)}, u32[]{:S(2)}, u32[]{:S(2)}) collective-permute-start(bf16[4,72,4608]{2,1,0:T(8,128)(2,1)} %get-tuple-element.21.refs_0_), channel_id=1, source_target_pairs={{0,1},{1,0},{2,3},{3,2},{4,5},{5,4},{6,7},{7,6},{8,9},{9,8},{10,11... | collective-permute-start | bytes 7962632 | tf_op jit(solution)/shard_map/ppermute | solution.py:548
  242.4 3.8 copy-start.6
  242.4 3.8 collective-permute-start.23
  243.4 107.9 %copy-start.7 = (bf16[4,144,1152]{2,1,0:T(8,128)(2,1)}, bf16[4,144,1152]{2,1,0:T(8,128)(2,1)S(1)}, u32[]{:S(2)}) copy-start(bf16[4,144,1152]{2,1,0:T(8,128)(2,1)S(1)} %collective-permute-done.21.refs_2_) | copy-start | bytes 3981316
  243.4 4.6 %collective-permute-start.24 = (bf16[4,144,1152]{2,1,0:T(8,128)(2,1)S(1)}, bf16[4,144,1152]{2,1,0:T(8,128)(2,1)S(1)}, u32[]{:S(2)}, u32[]{:S(2)}) collective-permute-start(bf16[4,144,1152]{2,1,0:T(8,128)(2,1)S(1)} %collective-permute-done.21.refs_2_), channel_id=1, source_target_pairs={{0,1},{1,0},{2,3},{3,2},{4,5},{5,4},{6,7},{7,6},{8,9},{9,8},{10,11... | collective-permute-start | bytes 3981320 | tf_op jit(solution)/shard_map/ppermute | solution.py:548
  243.5 2.7 copy-start.8
  243.5 18.1 %collective-permute-start.15 = (bf16[4,144,1152]{2,1,0:T(8,128)(2,1)S(1)}, bf16[4,144,1152]{2,1,0:T(8,128)(2,1)S(1)}, u32[]{:S(2)}, u32[]{:S(2)}) collective-permute-start(bf16[4,144,1152]{2,1,0:T(8,128)(2,1)S(1)} %collective-permute-done.14.refs_0_), channel_id=1, source_target_pairs={{0,2},{1,9},{2,4},{3,11},{4,6},{5,13},{6,0},{7,15},{8,10},{9,17},{... | collective-permute-start | bytes 3981320 | tf_op jit(solution)/shard_map/ppermute | solution.py:548
  244.1 109.3 %copy-start.9 = (bf16[4,144,1152]{2,1,0:T(8,128)(2,1)}, bf16[4,144,1152]{2,1,0:T(8,128)(2,1)S(1)}, u32[]{:S(2)}) copy-start(bf16[4,144,1152]{2,1,0:T(8,128)(2,1)S(1)} %collective-permute-done.25.refs_7_) | copy-start | bytes 3981316
  244.1 17.5 %collective-permute-start.18 = (bf16[4,144,1152]{2,1,0:T(8,128)(2,1)S(1)}, bf16[4,144,1152]{2,1,0:T(8,128)(2,1)S(1)}, u32[]{:S(2)}, u32[]{:S(2)}) collective-permute-start(bf16[4,144,1152]{2,1,0:T(8,128)(2,1)S(1)} %collective-permute-done.17.refs_3_), channel_id=1, source_target_pairs={{0,6},{1,25},{2,0},{3,27},{4,2},{5,29},{6,4},{7,31},{8,14},{9,1},{... | collective-permute-start | bytes 3981320 | tf_op jit(solution)/shard_map/ppermute | solution.py:548
  246.2 107.2 %copy-start.10 = (bf16[4,144,1152]{2,1,0:T(8,128)(2,1)}, bf16[4,144,1152]{2,1,0:T(8,128)(2,1)S(1)}, u32[]{:S(2)}) copy-start(bf16[4,144,1152]{2,1,0:T(8,128)(2,1)S(1)} %collective-permute-done.23.refs_5_) | copy-start | bytes 3981316
  246.2 43.4 %collective-permute-start.7 = (bf16[4,72,4608]{2,1,0:T(8,128)(2,1)}, bf16[4,72,4608]{2,1,0:T(8,128)(2,1)S(1)}, u32[]{:S(2)}, u32[]{:S(2)}) collective-permute-start(bf16[4,72,4608]{2,1,0:T(8,128)(2,1)} %get-tuple-element.21.refs_0_), channel_id=1, source_target_pairs={{0,6},{1,25},{2,0},{3,27},{4,2},{5,29},{6,4},{7,31},{8,14},{9,1},{... | collective-permute-start | bytes 7962632 | tf_op jit(solution)/shard_map/ppermute | solution.py:548
  248.0 105.5 %copy-start.11 = (bf16[4,144,1152]{2,1,0:T(8,128)(2,1)}, bf16[4,144,1152]{2,1,0:T(8,128)(2,1)S(1)}, u32[]{:S(2)}) copy-start(bf16[4,144,1152]{2,1,0:T(8,128)(2,1)S(1)} %collective-permute-done.24.refs_6_) | copy-start | bytes 3981316
  248.0 43.0 %collective-permute-start.10 = (bf16[4,72,4608]{2,1,0:T(8,128)(2,1)}, bf16[4,72,4608]{2,1,0:T(8,128)(2,1)}, u32[]{:S(2)}, u32[]{:S(2)}) collective-permute-start(bf16[4,72,4608]{2,1,0:T(8,128)(2,1)} %get-tuple-element.21.refs_0_), channel_id=1, source_target_pairs={{0,2},{1,9},{2,4},{3,11},{4,6},{5,13},{6,0},{7,15},{8,10},{9,17},{... | collective-permute-start | bytes 7962632 | tf_op jit(solution)/shard_map/ppermute | solution.py:548
  261.6 91.8 %copy-start.14 = (bf16[4,144,1152]{2,1,0:T(8,128)(2,1)}, bf16[4,144,1152]{2,1,0:T(8,128)(2,1)S(1)}, u32[]{:S(2)}) copy-start(bf16[4,144,1152]{2,1,0:T(8,128)(2,1)S(1)} %collective-permute-done.15.refs_0_) | copy-start | bytes 3981316
  261.6 57.0 %collective-permute-start = (bf16[4,72,4608]{2,1,0:T(8,128)(2,1)}, bf16[4,72,4608]{2,1,0:T(8,128)(2,1)}, u32[]{:S(2)}, u32[]{:S(2)}) collective-permute-start(bf16[4,72,4608]{2,1,0:T(8,128)(2,1)} %get-tuple-element.20.refs_0_), channel_id=1, source_target_pairs={{0,2},{1,9},{2,4},{3,11},{4,6},{5,13},{6,0},{7,15},{8,10},{9,17},{... | collective-permute-start | bytes 7962632 | tf_op jit(solution)/shard_map/ppermute | solution.py:548
  261.7 91.8 %copy-start.15 = (bf16[4,144,1152]{2,1,0:T(8,128)(2,1)}, bf16[4,144,1152]{2,1,0:T(8,128)(2,1)S(1)}, u32[]{:S(2)}) copy-start(bf16[4,144,1152]{2,1,0:T(8,128)(2,1)S(1)} %collective-permute-done.18.refs_1_) | copy-start | bytes 3981316
  261.7 56.9 %collective-permute-start.6 = (bf16[4,72,4608]{2,1,0:T(8,128)(2,1)}, bf16[4,72,4608]{2,1,0:T(8,128)(2,1)S(1)}, u32[]{:S(2)}, u32[]{:S(2)}) collective-permute-start(bf16[4,72,4608]{2,1,0:T(8,128)(2,1)} %get-tuple-element.20.refs_0_), channel_id=1, source_target_pairs={{0,1},{1,0},{2,3},{3,2},{4,5},{5,4},{6,7},{7,6},{8,9},{9,8},{10,11... | collective-permute-start | bytes 7962632 | tf_op jit(solution)/shard_map/ppermute | solution.py:548
  263.0 1.7 copy-start.2
  263.0 57.0 %collective-permute-start.3 = (bf16[4,72,4608]{2,1,0:T(8,128)(2,1)}, bf16[4,72,4608]{2,1,0:T(8,128)(2,1)}, u32[]{:S(2)}, u32[]{:S(2)}) collective-permute-start(bf16[4,72,4608]{2,1,0:T(8,128)(2,1)} %get-tuple-element.20.refs_0_), channel_id=1, source_target_pairs={{0,6},{1,25},{2,0},{3,27},{4,2},{5,29},{6,4},{7,31},{8,14},{9,1},{... | collective-permute-start | bytes 7962632 | tf_op jit(solution)/shard_map/ppermute | solution.py:548
  289.6 1.6 copy-start
  289.6 35.3 %collective-permute-start.12 = (bf16[4,72,4608]{2,1,0:T(8,128)(2,1)S(1)}, bf16[4,72,4608]{2,1,0:T(8,128)(2,1)S(1)}, u32[]{:S(2)}, u32[]{:S(2)}) collective-permute-start(bf16[4,72,4608]{2,1,0:T(8,128)(2,1)S(1)} %collective-permute-done.7.refs_1_), channel_id=1, source_target_pairs={{0,1},{1,0},{2,3},{3,2},{4,5},{5,4},{6,7},{7,6},{8,9},{9,8},{10,11... | collective-permute-start | bytes 7962632 | tf_op jit(solution)/shard_map/ppermute | solution.py:548
  291.2 55.3 %collective-permute-start.8 = (bf16[4,72,4608]{2,1,0:T(8,128)(2,1)S(1)}, bf16[4,72,4608]{2,1,0:T(8,128)(2,1)}, u32[]{:S(2)}, u32[]{:S(2)}) collective-permute-start(bf16[4,72,4608]{2,1,0:T(8,128)(2,1)S(1)} %collective-permute-done.7.refs_1_), channel_id=1, source_target_pairs={{0,6},{1,25},{2,0},{3,27},{4,2},{5,29},{6,4},{7,31},{8,14},{9,1},{... | collective-permute-start | bytes 7962632 | tf_op jit(solution)/shard_map/ppermute | solution.py:548
  318.6 32.7 %collective-permute-start.1 = (bf16[4,72,4608]{2,1,0:T(8,128)(2,1)}, bf16[4,72,4608]{2,1,0:T(8,128)(2,1)}, u32[]{:S(2)}, u32[]{:S(2)}) collective-permute-start(bf16[4,72,4608]{2,1,0:T(8,128)(2,1)} %collective-permute-done.refs_0_), channel_id=1, source_target_pairs={{0,2},{1,9},{2,4},{3,11},{4,6},{5,13},{6,0},{7,15},{8,10},{9,17},{... | collective-permute-start | bytes 7962632 | tf_op jit(solution)/shard_map/ppermute | solution.py:548
  318.6 29.1 %copy-start.3 = (bf16[4,72,4608]{2,1,0:T(8,128)(2,1)}, bf16[4,72,4608]{2,1,0:T(8,128)(2,1)S(1)}, u32[]{:S(2)}) copy-start(bf16[4,72,4608]{2,1,0:T(8,128)(2,1)S(1)} %collective-permute-done.6.refs_1_) | copy-start | bytes 7962628
  318.6 4.0 collective-permute-start.16
  320.0 4.6 %collective-permute-start.19 = (bf16[4,144,1152]{2,1,0:T(8,128)(2,1)S(1)}, bf16[4,144,1152]{2,1,0:T(8,128)(2,1)S(1)}, u32[]{:S(2)}, u32[]{:S(2)}) collective-permute-start(bf16[4,144,1152]{2,1,0:T(8,128)(2,1)S(1)} %collective-permute-done.18.refs_1_), channel_id=1, source_target_pairs={{0,1},{1,0},{2,3},{3,2},{4,5},{5,4},{6,7},{7,6},{8,9},{9,8},{10,11... | collective-permute-start | bytes 3981320 | tf_op jit(solution)/shard_map/ppermute | solution.py:548
  322.7 30.8 %copy-start.16 = (bf16[4,144,1152]{2,1,0:T(8,128)(2,1)}, bf16[4,144,1152]{2,1,0:T(8,128)(2,1)S(1)}, u32[]{:S(2)}) copy-start(bf16[4,144,1152]{2,1,0:T(8,128)(2,1)S(1)} %collective-permute-done.16.refs_0_) | copy-start | bytes 3981316
  322.7 67.9 %collective-permute-start.11 = (bf16[4,72,4608]{2,1,0:T(8,128)(2,1)}, bf16[4,72,4608]{2,1,0:T(8,128)(2,1)}, u32[]{:S(2)}, u32[]{:S(2)}) collective-permute-start(bf16[4,72,4608]{2,1,0:T(8,128)(2,1)} %collective-permute-done.10.refs_0_), channel_id=1, source_target_pairs={{0,1},{1,0},{2,3},{3,2},{4,5},{5,4},{6,7},{7,6},{8,9},{9,8},{10,11... | collective-permute-start | bytes 7962632 | tf_op jit(solution)/shard_map/ppermute | solution.py:548
  324.6 28.9 %copy-start.17 = (bf16[4,144,1152]{2,1,0:T(8,128)(2,1)}, bf16[4,144,1152]{2,1,0:T(8,128)(2,1)S(1)}, u32[]{:S(2)}) copy-start(bf16[4,144,1152]{2,1,0:T(8,128)(2,1)S(1)} %collective-permute-done.19.refs_1_) | copy-start | bytes 3981316
  324.6 74.2 %collective-permute-start.4 = (bf16[4,72,4608]{2,1,0:T(8,128)(2,1)}, bf16[4,72,4608]{2,1,0:T(8,128)(2,1)}, u32[]{:S(2)}, u32[]{:S(2)}) collective-permute-start(bf16[4,72,4608]{2,1,0:T(8,128)(2,1)} %collective-permute-done.refs_0_), channel_id=1, source_target_pairs={{0,1},{1,0},{2,3},{3,2},{4,5},{5,4},{6,7},{7,6},{8,9},{9,8},{10,11... | collective-permute-start | bytes 7962632 | tf_op jit(solution)/shard_map/ppermute | solution.py:548
  324.9 21.5 %copy-start.1 = (bf16[4,72,4608]{2,1,0:T(8,128)(2,1)}, bf16[4,72,4608]{2,1,0:T(8,128)(2,1)S(1)}, u32[]{:S(2)}) copy-start(bf16[4,72,4608]{2,1,0:T(8,128)(2,1)S(1)} %collective-permute-done.12.refs_3_) | copy-start | bytes 7962628
  325.0 73.9 %collective-permute-start.5 = (bf16[4,72,4608]{2,1,0:T(8,128)(2,1)}, bf16[4,72,4608]{2,1,0:T(8,128)(2,1)}, u32[]{:S(2)}, u32[]{:S(2)}) collective-permute-start(bf16[4,72,4608]{2,1,0:T(8,128)(2,1)} %collective-permute-done.3.refs_1_), channel_id=1, source_target_pairs={{0,1},{1,0},{2,3},{3,2},{4,5},{5,4},{6,7},{7,6},{8,9},{9,8},{10,11... | collective-permute-start | bytes 7962632 | tf_op jit(solution)/shard_map/ppermute | solution.py:548
  346.5 60.5 %collective-permute-start.9 = (bf16[4,72,4608]{2,1,0:T(8,128)(2,1)}, bf16[4,72,4608]{2,1,0:T(8,128)(2,1)}, u32[]{:S(2)}, u32[]{:S(2)}) collective-permute-start(bf16[4,72,4608]{2,1,0:T(8,128)(2,1)} %collective-permute-done.8.refs_0_), channel_id=1, source_target_pairs={{0,1},{1,0},{2,3},{3,2},{4,5},{5,4},{6,7},{7,6},{8,9},{9,8},{10,11... | collective-permute-start | bytes 7962632 | tf_op jit(solution)/shard_map/ppermute | solution.py:548
  351.3 60.0 %collective-permute-start.2 = (bf16[4,72,4608]{2,1,0:T(8,128)(2,1)}, bf16[4,72,4608]{2,1,0:T(8,128)(2,1)}, u32[]{:S(2)}, u32[]{:S(2)}) collective-permute-start(bf16[4,72,4608]{2,1,0:T(8,128)(2,1)} %collective-permute-done.1.refs_0_), channel_id=1, source_target_pairs={{0,1},{1,0},{2,3},{3,2},{4,5},{5,4},{6,7},{7,6},{8,9},{9,8},{10,11... | collective-permute-start | bytes 7962632 | tf_op jit(solution)/shard_map/ppermute | solution.py:548

commit v4 on v3

--- a/solution.py
+++ b/solution.py
@@ -321,7 +321,7 @@
             wait_for(w_new.at[i], f_send.at[i])
 
             def forward(part):
-                low, high = part(fm, 0, top), part(fp, top, rows - top)
+                low, high = part(fm, 0, rows - top), part(fp, rows - top, top)
                 send(low, low, n_send.at[i], no_sem.at[i], right).start()
                 send(high, high, f_send.at[i], no_sem.at[i], left).start()
 
@@ -344,8 +344,8 @@
         wait_for(g.at[i, core], g_send.at[i])
         wait_for(w_new.at[i], n_own.at[i])
         wait_for(w_new.at[i], no_sem.at[i])
-        wait_for(w_new.at[i, pl.ds(0, top)], n_send.at[i])
-        wait_for(w_new.at[i, pl.ds(top, rows - top)], f_send.at[i])
+        wait_for(w_new.at[i, pl.ds(0, rows - top)], n_send.at[i])
+        wait_for(w_new.at[i, pl.ds(0, top)], f_send.at[i])
 
         @pl.when(i < wide)
         def _():

time: 416 us -> 414 us (level)
  transfers between devices with their start and end apart: 28 -> 28, of which waited for: 10 -> 9; matrix products, arithmetic and copies ran while one was open for 0% -> 0% of each run, Pallas kernels for 14% -> 14%
where the time goes in v4:
time: 414 us
  Pallas kernels  268 us (65%)
  waiting for transfers between devices  114 us (28%)
  starting transfers between devices  28.2 us (7%)
    pallas_call x1, Pallas kernels, reduce_and_step(): pl.pallas_call(functools.partial(reduce_kernel, side, quarters, rows, col...  207 us
    ppermute x28, waiting for transfers between devices, move(): return lax.ppermute(x, 'dp', pairs)  114 us
    pallas_call x10, Pallas kernels, place(): pl.pallas_call(functools.partial(place_kernel, side, [job[1:] for job in...  51.9 us
    ppermute x28, starting transfers between devices, move(): return lax.ppermute(x, 'dp', pairs)  28.2 us
    pallas_call x1, Pallas kernels, moments(): pl.pallas_call(functools.partial(moments_kernel, side, quarters, rows, co...  10 us
  transfers between devices with their start and end apart: 28, of which 9 were waited for; matrix products, arithmetic and copies ran while one was open for 0% of the time, Pallas kernels for 14%

profile of v4, /device:TPU:97, one launch (start us, length us, event | category | flops | bytes accessed | tf_op | source)
XLA Modules:
  0.0 413.5 jit_solution(11771311911457998054)
XLA Ops:
  0.6 206.5 %reduce_and_step.1 = (bf16[12,2,72,1152]{3,2,1,0:T(8,128)(2,1)}, bf16[4,72,4608]{2,1,0:T(8,128)(2,1)}, bf16[4,72,4608]{2,1,0:T(8,128)(2,1)}, bf16[4,144,1152]{2,1,0:T(8,128)(2,1)}, bf16[4,144,1152]{2,1,0:T(8,128)(2,1)}) custom-call(bf16[1,2,1152,4608]{3,2,1,0:T(8,128)(2,1)} %refs_0_.1, bf16[1,2,1152,4608]{3,2,1,0:T(8,128)(2,1)} %refs_1_.1, ...), custom_call_target="tpu_custom_call" | custom-call | tf_op jit(solution)/shard_map/reduce_and_step/pallas_call | solution.py:373
  207.2 0.7 collective-permute-start.26
  207.9 0.8 collective-permute-start.14
  208.7 1.9 collective-permute-start.17
  210.6 0.7 collective-permute-start.27
  211.2 0.8 collective-permute-start.20
  212.0 0.0 collective-permute-done.26.refs_2_
  212.1 1.9 collective-permute-start.21
  213.9 12.3 %collective-permute-done.14.refs_0_ = bf16[4,144,1152]{2,1,0:T(8,128)(2,1)S(1)} collective-permute-done((bf16[4,144,1152]{2,1,0:T(8,128)(2,1)}, bf16[4,144,1152]{2,1,0:T(8,128)(2,1)S(1)}, u32[]{:S(2)}, u32[]{:S(2)}) %collective-permute-start.14) | collective-permute-done | bytes 1327136 | tf_op jit(solution)/shard_map/ppermute | solution.py:548
  226.2 1.0 collective-permute-start.22
  227.2 0.0 collective-permute-done.17.refs_3_
  227.2 0.1 collective-permute-start.25
  227.3 0.0 collective-permute-done.27.refs_3_
  227.3 1.2 copy-done.13
  228.5 0.6 collective-permute-start.13
  229.1 11.3 %collective-permute-done.20.refs_1_ = bf16[4,144,1152]{2,1,0:T(8,128)(2,1)S(1)} collective-permute-done((bf16[4,144,1152]{2,1,0:T(8,128)(2,1)}, bf16[4,144,1152]{2,1,0:T(8,128)(2,1)S(1)}, u32[]{:S(2)}, u32[]{:S(2)}) %collective-permute-start.20) | collective-permute-done | bytes 1327136 | tf_op jit(solution)/shard_map/ppermute | solution.py:548
  240.5 1.0 collective-permute-start.23
  241.4 0.1 collective-permute-start.24
  241.6 0.8 collective-permute-start.15
  242.4 1.9 collective-permute-start.18
  244.2 0.0 collective-permute-done.23.refs_5_
  244.3 2.1 collective-permute-start.7
  246.3 0.5 collective-permute-start.10
  246.8 12.9 %collective-permute-done.15.refs_0_ = bf16[4,144,1152]{2,1,0:T(8,128)(2,1)S(1)} collective-permute-done((bf16[4,144,1152]{2,1,0:T(8,128)(2,1)S(1)}, bf16[4,144,1152]{2,1,0:T(8,128)(2,1)S(1)}, u32[]{:S(2)}, u32[]{:S(2)}) %collective-permute-start.15) | collective-permute-done | bytes 1327136 | tf_op jit(solution)/shard_map/ppermute | solution.py:548
  259.7 0.0 collective-permute-start
  259.7 0.0 collective-permute-done.18.refs_1_
  259.7 1.4 collective-permute-start.6
  261.1 2.2 collective-permute-start.3
  263.3 24.5 %collective-permute-done.7.refs_1_ = bf16[4,72,4608]{2,1,0:T(8,128)(2,1)S(1)} collective-permute-done((bf16[4,72,4608]{2,1,0:T(8,128)(2,1)}, bf16[4,72,4608]{2,1,0:T(8,128)(2,1)S(1)}, u32[]{:S(2)}, u32[]{:S(2)}) %collective-permute-start.7) | collective-permute-done | bytes 2654240 | tf_op jit(solution)/shard_map/ppermute | solution.py:548
  287.8 1.2 collective-permute-start.12
  289.1 0.3 copy-done
  289.4 3.1 collective-permute-start.8
  292.5 24.2 %collective-permute-done.refs_0_ = bf16[4,72,4608]{2,1,0:T(8,128)(2,1)} collective-permute-done((bf16[4,72,4608]{2,1,0:T(8,128)(2,1)}, bf16[4,72,4608]{2,1,0:T(8,128)(2,1)}, u32[]{:S(2)}, u32[]{:S(2)}) %collective-permute-start) | collective-permute-done | bytes 2654240 | tf_op jit(solution)/shard_map/ppermute | solution.py:548
  316.7 0.0 collective-permute-start.1
  316.7 0.0 collective-permute-done.6.refs_1_
  316.7 1.4 collective-permute-start.16
  318.0 0.0 collective-permute-done.3.refs_1_
  318.1 0.1 collective-permute-start.19
  318.2 2.5 collective-permute-done.16.refs_0_
  320.7 0.4 collective-permute-start.11
  321.1 1.5 collective-permute-done.19.refs_1_
  322.6 0.4 collective-permute-start.4
  323.0 0.0 collective-permute-done.12.refs_3_
  323.0 0.1 collective-permute-start.5
  323.2 21.6 %collective-permute-done.8.refs_0_ = bf16[4,72,4608]{2,1,0:T(8,128)(2,1)} collective-permute-done((bf16[4,72,4608]{2,1,0:T(8,128)(2,1)S(1)}, bf16[4,72,4608]{2,1,0:T(8,128)(2,1)}, u32[]{:S(2)}, u32[]{:S(2)}) %collective-permute-start.8) | collective-permute-done | bytes 2654240 | tf_op jit(solution)/shard_map/ppermute | solution.py:548
  344.7 1.1 collective-permute-start.9
  345.8 3.5 collective-permute-done.1.refs_0_
  349.4 2.1 collective-permute-start.2
  351.5 10.0 %moments.1 = (f32[36,2,4608]{2,1,0:T(2,128)}, f32[36,2,4608]{2,1,0:T(2,128)}, f32[2,144,1152]{2,1,0:T(8,128)}, f32[36,2,4608]{2,1,0:T(2,128)}, f32[36,2,4608]{2,1,0:T(2,128)}, /*index=5*/f32[2,144,1152]{2,1,0:T(8,128)}) custom-call(bf16[12,2,72,1152]{3,2,1,0:T(8,128)(2,1)} %get-tuple-element.24.refs_0_, f32[36,2,4608]{2,1,0:T(2,128)} %bitcast.9, ...), custom_call_target="tpu_custom_call" | custom-call | flops 31850496 | bytes 15925248 | tf_op jit(solution)/shard_map/moments/pallas_call | solution.py:471
  361.5 4.4 %place.16.refs_8_ = bf16[2,4608,1152]{2,1,0:T(8,128)(2,1)} custom-call(bf16[4,144,1152]{2,1,0:T(8,128)(2,1)} %get-tuple-element.22.refs_0_, bf16[4,144,1152]{2,1,0:T(8,128)(2,1)} %get-tuple-element.23.refs_1_, bf16[4,144,1152]{2,1,0:T(8,128)(2,1)} %copy-done.12, bf16[4,144,1152]{2,1,0:T(8,128)(2,1)} %copy-done.13), custom_call_target="tpu_custom_call" | custom-call | flops 10616832 | bytes 10616832 | tf_op jit(solution)/shard_map/place/pallas_call | solution.py:518
  365.9 8.5 %place.17.refs_2_ = bf16[2,4608,1152]{2,1,0:T(8,128)(2,1)} custom-call(bf16[4,144,1152]{2,1,0:T(8,128)(2,1)} %copy-done.4, bf16[4,144,1152]{2,1,0:T(8,128)(2,1)} %copy-done.6, bf16[4,144,1152]{2,1,0:T(8,128)(2,1)} %copy-done.7, bf16[4,144,1152]{2,1,0:T(8,128)(2,1)} %copy-done.5, bf16[4,144,1152]{2,1,0:T(8,128)(2,1)} %copy-done.8, ...), custom_call_target="tpu_custom_call", output_to_operand_aliasing={{}: (8, {})} | custom-call | flops 21233664 | bytes 21233664 | tf_op jit(solution)/shard_map/place/pallas_call | solution.py:518
  374.4 2.9 place.18.refs_2_
  377.3 4.2 %place.13.refs_4_ = bf16[2,1152,4608]{2,1,0:T(8,128)(2,1)} custom-call(bf16[4,72,4608]{2,1,0:T(8,128)(2,1)} %get-tuple-element.21.refs_0_, bf16[4,72,4608]{2,1,0:T(8,128)(2,1)} %copy-done.2), custom_call_target="tpu_custom_call" | custom-call | flops 10616832 | bytes 10616832 | tf_op jit(solution)/shard_map/place/pallas_call | solution.py:518
  381.5 4.2 %place.10.refs_4_ = bf16[2,1152,4608]{2,1,0:T(8,128)(2,1)} custom-call(bf16[4,72,4608]{2,1,0:T(8,128)(2,1)} %get-tuple-element.20.refs_0_, bf16[4,72,4608]{2,1,0:T(8,128)(2,1)} %copy-done.3), custom_call_target="tpu_custom_call" | custom-call | flops 10616832 | bytes 10616832 | tf_op jit(solution)/shard_map/place/pallas_call | solution.py:518
  385.8 2.9 place.19
  388.7 0.0 collective-permute-done.11.refs_2_
  388.7 8.2 %place.14.refs_2_ = bf16[2,1152,4608]{2,1,0:T(8,128)(2,1)} custom-call(bf16[4,72,4608]{2,1,0:T(8,128)(2,1)} %collective-permute-done.10.refs_0_, bf16[4,72,4608]{2,1,0:T(8,128)(2,1)} %copy-done, bf16[4,72,4608]{2,1,0:T(8,128)(2,1)} %collective-permute-done.11.refs_2_, bf16[4,72,4608]{2,1,0:T(8,128)(2,1)} %copy-done.1, ...), custom_call_target="tpu_custom_call", output_to_operand_aliasing={{}: (4, {})} | custom-call | flops 21233664 | bytes 21233664 | tf_op jit(solution)/shard_map/place/pallas_call | solution.py:518
  396.9 0.0 collective-permute-done.4.refs_2_
  396.9 0.0 collective-permute-done.5.refs_3_
  396.9 8.2 %place.11.refs_2_ = bf16[2,1152,4608]{2,1,0:T(8,128)(2,1)} custom-call(bf16[4,72,4608]{2,1,0:T(8,128)(2,1)} %collective-permute-done.refs_0_, bf16[4,72,4608]{2,1,0:T(8,128)(2,1)} %collective-permute-done.3.refs_1_, bf16[4,72,4608]{2,1,0:T(8,128)(2,1)} %collective-permute-done.4.refs_2_, ...), custom_call_target="tpu_custom_call", output_to_operand_aliasing={{}: (4, {})} | custom-call | flops 21233664 | bytes 21233664 | tf_op jit(solution)/shard_map/place/pallas_call | solution.py:518
  405.1 0.0 collective-permute-done.9.refs_1_
  405.1 4.2 %place.15 = bf16[2,1152,4608]{2,1,0:T(8,128)(2,1)} custom-call(bf16[4,72,4608]{2,1,0:T(8,128)(2,1)} %collective-permute-done.8.refs_0_, bf16[4,72,4608]{2,1,0:T(8,128)(2,1)} %collective-permute-done.9.refs_1_, bf16[2,1152,4608]{2,1,0:T(8,128)(2,1)} %place.14.refs_2_), custom_call_target="tpu_custom_call", output_to_operand_aliasing={{}: (2, {})} | custom-call | flops 10616832 | bytes 10616832 | tf_op jit(solution)/shard_map/place/pallas_call | solution.py:518
  409.3 0.0 collective-permute-done.2.refs_1_
  409.3 4.2 %place.12 = bf16[2,1152,4608]{2,1,0:T(8,128)(2,1)} custom-call(bf16[4,72,4608]{2,1,0:T(8,128)(2,1)} %collective-permute-done.1.refs_0_, bf16[4,72,4608]{2,1,0:T(8,128)(2,1)} %collective-permute-done.2.refs_1_, bf16[2,1152,4608]{2,1,0:T(8,128)(2,1)} %place.11.refs_2_), custom_call_target="tpu_custom_call", output_to_operand_aliasing={{}: (2, {})} | custom-call | flops 10616832 | bytes 10616832 | tf_op jit(solution)/shard_map/place/pallas_call | solution.py:518
  (40 shorter events, 0.1 us)
Async XLA Ops:
  207.2 4.9 %collective-permute-start.26 = (bf16[4,144,1152]{2,1,0:T(8,128)(2,1)}, bf16[4,144,1152]{2,1,0:T(8,128)(2,1)S(1)}, u32[]{:S(2)}, u32[]{:S(2)}) collective-permute-start(bf16[4,144,1152]{2,1,0:T(8,128)(2,1)} %get-tuple-element.22.refs_0_), channel_id=1, source_target_pairs={{0,1},{1,0},{2,3},{3,2},{4,5},{5,4},{6,7},{7,6},{8,9},{9,8},{10,11... | collective-permute-start | bytes 3981320 | tf_op jit(solution)/shard_map/ppermute | solution.py:548
  207.9 18.3 %collective-permute-start.14 = (bf16[4,144,1152]{2,1,0:T(8,128)(2,1)}, bf16[4,144,1152]{2,1,0:T(8,128)(2,1)S(1)}, u32[]{:S(2)}, u32[]{:S(2)}) collective-permute-start(bf16[4,144,1152]{2,1,0:T(8,128)(2,1)} %get-tuple-element.22.refs_0_), channel_id=1, source_target_pairs={{0,2},{1,9},{2,4},{3,11},{4,6},{5,13},{6,0},{7,15},{8,10},{9,17},{... | collective-permute-start | bytes 3981320 | tf_op jit(solution)/shard_map/ppermute | solution.py:548
  208.7 18.5 %collective-permute-start.17 = (bf16[4,144,1152]{2,1,0:T(8,128)(2,1)}, bf16[4,144,1152]{2,1,0:T(8,128)(2,1)S(1)}, u32[]{:S(2)}, u32[]{:S(2)}) collective-permute-start(bf16[4,144,1152]{2,1,0:T(8,128)(2,1)} %get-tuple-element.23.refs_1_), channel_id=1, source_target_pairs={{0,6},{1,25},{2,0},{3,27},{4,2},{5,29},{6,4},{7,31},{8,14},{9,1},{... | collective-permute-start | bytes 3981320 | tf_op jit(solution)/shard_map/ppermute | solution.py:548
  210.6 16.8 %collective-permute-start.27 = (bf16[4,144,1152]{2,1,0:T(8,128)(2,1)}, bf16[4,144,1152]{2,1,0:T(8,128)(2,1)S(1)}, u32[]{:S(2)}, u32[]{:S(2)}) collective-permute-start(bf16[4,144,1152]{2,1,0:T(8,128)(2,1)} %get-tuple-element.23.refs_1_), channel_id=1, source_target_pairs={{0,1},{1,0},{2,3},{3,2},{4,5},{5,4},{6,7},{7,6},{8,9},{9,8},{10,11... | collective-permute-start | bytes 3981320 | tf_op jit(solution)/shard_map/ppermute | solution.py:548
  211.2 29.2 %collective-permute-start.20 = (bf16[4,144,1152]{2,1,0:T(8,128)(2,1)}, bf16[4,144,1152]{2,1,0:T(8,128)(2,1)S(1)}, u32[]{:S(2)}, u32[]{:S(2)}) collective-permute-start(bf16[4,144,1152]{2,1,0:T(8,128)(2,1)} %get-tuple-element.23.refs_1_), channel_id=1, source_target_pairs={{0,2},{1,9},{2,4},{3,11},{4,6},{5,13},{6,0},{7,15},{8,10},{9,17},{... | collective-permute-start | bytes 3981320 | tf_op jit(solution)/shard_map/ppermute | solution.py:548
  212.1 1.9 copy-start.12
  212.1 29.4 %collective-permute-start.21 = (bf16[4,144,1152]{2,1,0:T(8,128)(2,1)}, bf16[4,144,1152]{2,1,0:T(8,128)(2,1)S(1)}, u32[]{:S(2)}, u32[]{:S(2)}) collective-permute-start(bf16[4,144,1152]{2,1,0:T(8,128)(2,1)} %get-tuple-element.22.refs_0_), channel_id=1, source_target_pairs={{0,6},{1,25},{2,0},{3,27},{4,2},{5,29},{6,4},{7,31},{8,14},{9,1},{... | collective-permute-start | bytes 3981320 | tf_op jit(solution)/shard_map/ppermute | solution.py:548
  226.2 33.5 %copy-start.4 = (bf16[4,144,1152]{2,1,0:T(8,128)(2,1)}, bf16[4,144,1152]{2,1,0:T(8,128)(2,1)S(1)}, u32[]{:S(2)}) copy-start(bf16[4,144,1152]{2,1,0:T(8,128)(2,1)S(1)} %collective-permute-done.14.refs_0_) | copy-start | bytes 3981316
  226.2 15.3 %collective-permute-start.22 = (bf16[4,144,1152]{2,1,0:T(8,128)(2,1)S(1)}, bf16[4,144,1152]{2,1,0:T(8,128)(2,1)S(1)}, u32[]{:S(2)}, u32[]{:S(2)}) collective-permute-start(bf16[4,144,1152]{2,1,0:T(8,128)(2,1)S(1)} %collective-permute-done.14.refs_0_), channel_id=1, source_target_pairs={{0,1},{1,0},{2,3},{3,2},{4,5},{5,4},{6,7},{7,6},{8,9},{9,8},{10,11... | collective-permute-start | bytes 3981320 | tf_op jit(solution)/shard_map/ppermute | solution.py:548
  227.2 32.5 %copy-start.5 = (bf16[4,144,1152]{2,1,0:T(8,128)(2,1)}, bf16[4,144,1152]{2,1,0:T(8,128)(2,1)S(1)}, u32[]{:S(2)}) copy-start(bf16[4,144,1152]{2,1,0:T(8,128)(2,1)S(1)} %collective-permute-done.17.refs_3_) | copy-start | bytes 3981316
  227.2 15.1 %collective-permute-start.25 = (bf16[4,144,1152]{2,1,0:T(8,128)(2,1)S(1)}, bf16[4,144,1152]{2,1,0:T(8,128)(2,1)S(1)}, u32[]{:S(2)}, u32[]{:S(2)}) collective-permute-start(bf16[4,144,1152]{2,1,0:T(8,128)(2,1)S(1)} %collective-permute-done.17.refs_3_), channel_id=1, source_target_pairs={{0,1},{1,0},{2,3},{3,2},{4,5},{5,4},{6,7},{7,6},{8,9},{9,8},{10,11... | collective-permute-start | bytes 3981320 | tf_op jit(solution)/shard_map/ppermute | solution.py:548
  227.3 1.2 copy-start.13
  228.5 32.6 %collective-permute-start.13 = (bf16[4,72,4608]{2,1,0:T(8,128)(2,1)}, bf16[4,72,4608]{2,1,0:T(8,128)(2,1)S(1)}, u32[]{:S(2)}, u32[]{:S(2)}) collective-permute-start(bf16[4,72,4608]{2,1,0:T(8,128)(2,1)} %get-tuple-element.21.refs_0_), channel_id=1, source_target_pairs={{0,1},{1,0},{2,3},{3,2},{4,5},{5,4},{6,7},{7,6},{8,9},{9,8},{10,11... | collective-permute-start | bytes 7962632 | tf_op jit(solution)/shard_map/ppermute | solution.py:548
  240.5 3.8 copy-start.6
  240.5 3.8 collective-permute-start.23
  241.4 107.9 %copy-start.7 = (bf16[4,144,1152]{2,1,0:T(8,128)(2,1)}, bf16[4,144,1152]{2,1,0:T(8,128)(2,1)S(1)}, u32[]{:S(2)}) copy-start(bf16[4,144,1152]{2,1,0:T(8,128)(2,1)S(1)} %collective-permute-done.21.refs_2_) | copy-start | bytes 3981316
  241.4 4.9 %collective-permute-start.24 = (bf16[4,144,1152]{2,1,0:T(8,128)(2,1)S(1)}, bf16[4,144,1152]{2,1,0:T(8,128)(2,1)S(1)}, u32[]{:S(2)}, u32[]{:S(2)}) collective-permute-start(bf16[4,144,1152]{2,1,0:T(8,128)(2,1)S(1)} %collective-permute-done.21.refs_2_), channel_id=1, source_target_pairs={{0,1},{1,0},{2,3},{3,2},{4,5},{5,4},{6,7},{7,6},{8,9},{9,8},{10,11... | collective-permute-start | bytes 3981320 | tf_op jit(solution)/shard_map/ppermute | solution.py:548
  241.6 2.7 copy-start.8
  241.6 18.1 %collective-permute-start.15 = (bf16[4,144,1152]{2,1,0:T(8,128)(2,1)S(1)}, bf16[4,144,1152]{2,1,0:T(8,128)(2,1)S(1)}, u32[]{:S(2)}, u32[]{:S(2)}) collective-permute-start(bf16[4,144,1152]{2,1,0:T(8,128)(2,1)S(1)} %collective-permute-done.14.refs_0_), channel_id=1, source_target_pairs={{0,2},{1,9},{2,4},{3,11},{4,6},{5,13},{6,0},{7,15},{8,10},{9,17},{... | collective-permute-start | bytes 3981320 | tf_op jit(solution)/shard_map/ppermute | solution.py:548
  242.4 109.1 %copy-start.9 = (bf16[4,144,1152]{2,1,0:T(8,128)(2,1)}, bf16[4,144,1152]{2,1,0:T(8,128)(2,1)S(1)}, u32[]{:S(2)}) copy-start(bf16[4,144,1152]{2,1,0:T(8,128)(2,1)S(1)} %collective-permute-done.25.refs_7_) | copy-start | bytes 3981316
  242.4 17.4 %collective-permute-start.18 = (bf16[4,144,1152]{2,1,0:T(8,128)(2,1)S(1)}, bf16[4,144,1152]{2,1,0:T(8,128)(2,1)S(1)}, u32[]{:S(2)}, u32[]{:S(2)}) collective-permute-start(bf16[4,144,1152]{2,1,0:T(8,128)(2,1)S(1)} %collective-permute-done.17.refs_3_), channel_id=1, source_target_pairs={{0,6},{1,25},{2,0},{3,27},{4,2},{5,29},{6,4},{7,31},{8,14},{9,1},{... | collective-permute-start | bytes 3981320 | tf_op jit(solution)/shard_map/ppermute | solution.py:548
  244.3 107.2 %copy-start.10 = (bf16[4,144,1152]{2,1,0:T(8,128)(2,1)}, bf16[4,144,1152]{2,1,0:T(8,128)(2,1)S(1)}, u32[]{:S(2)}) copy-start(bf16[4,144,1152]{2,1,0:T(8,128)(2,1)S(1)} %collective-permute-done.23.refs_5_) | copy-start | bytes 3981316
  244.3 43.6 %collective-permute-start.7 = (bf16[4,72,4608]{2,1,0:T(8,128)(2,1)}, bf16[4,72,4608]{2,1,0:T(8,128)(2,1)S(1)}, u32[]{:S(2)}, u32[]{:S(2)}) collective-permute-start(bf16[4,72,4608]{2,1,0:T(8,128)(2,1)} %get-tuple-element.21.refs_0_), channel_id=1, source_target_pairs={{0,6},{1,25},{2,0},{3,27},{4,2},{5,29},{6,4},{7,31},{8,14},{9,1},{... | collective-permute-start | bytes 7962632 | tf_op jit(solution)/shard_map/ppermute | solution.py:548
  246.3 105.1 %copy-start.11 = (bf16[4,144,1152]{2,1,0:T(8,128)(2,1)}, bf16[4,144,1152]{2,1,0:T(8,128)(2,1)S(1)}, u32[]{:S(2)}) copy-start(bf16[4,144,1152]{2,1,0:T(8,128)(2,1)S(1)} %collective-permute-done.24.refs_6_) | copy-start | bytes 3981316
  246.3 42.7 %collective-permute-start.10 = (bf16[4,72,4608]{2,1,0:T(8,128)(2,1)}, bf16[4,72,4608]{2,1,0:T(8,128)(2,1)}, u32[]{:S(2)}, u32[]{:S(2)}) collective-permute-start(bf16[4,72,4608]{2,1,0:T(8,128)(2,1)} %get-tuple-element.21.refs_0_), channel_id=1, source_target_pairs={{0,2},{1,9},{2,4},{3,11},{4,6},{5,13},{6,0},{7,15},{8,10},{9,17},{... | collective-permute-start | bytes 7962632 | tf_op jit(solution)/shard_map/ppermute | solution.py:548
  259.7 91.8 %copy-start.14 = (bf16[4,144,1152]{2,1,0:T(8,128)(2,1)}, bf16[4,144,1152]{2,1,0:T(8,128)(2,1)S(1)}, u32[]{:S(2)}) copy-start(bf16[4,144,1152]{2,1,0:T(8,128)(2,1)S(1)} %collective-permute-done.15.refs_0_) | copy-start | bytes 3981316
  259.7 57.0 %collective-permute-start = (bf16[4,72,4608]{2,1,0:T(8,128)(2,1)}, bf16[4,72,4608]{2,1,0:T(8,128)(2,1)}, u32[]{:S(2)}, u32[]{:S(2)}) collective-permute-start(bf16[4,72,4608]{2,1,0:T(8,128)(2,1)} %get-tuple-element.20.refs_0_), channel_id=1, source_target_pairs={{0,2},{1,9},{2,4},{3,11},{4,6},{5,13},{6,0},{7,15},{8,10},{9,17},{... | collective-permute-start | bytes 7962632 | tf_op jit(solution)/shard_map/ppermute | solution.py:548
  259.7 91.8 %copy-start.15 = (bf16[4,144,1152]{2,1,0:T(8,128)(2,1)}, bf16[4,144,1152]{2,1,0:T(8,128)(2,1)S(1)}, u32[]{:S(2)}) copy-start(bf16[4,144,1152]{2,1,0:T(8,128)(2,1)S(1)} %collective-permute-done.18.refs_1_) | copy-start | bytes 3981316
  259.7 56.9 %collective-permute-start.6 = (bf16[4,72,4608]{2,1,0:T(8,128)(2,1)}, bf16[4,72,4608]{2,1,0:T(8,128)(2,1)S(1)}, u32[]{:S(2)}, u32[]{:S(2)}) collective-permute-start(bf16[4,72,4608]{2,1,0:T(8,128)(2,1)} %get-tuple-element.20.refs_0_), channel_id=1, source_target_pairs={{0,1},{1,0},{2,3},{3,2},{4,5},{5,4},{6,7},{7,6},{8,9},{9,8},{10,11... | collective-permute-start | bytes 7962632 | tf_op jit(solution)/shard_map/ppermute | solution.py:548
  261.1 2.2 copy-start.2
  261.1 57.0 %collective-permute-start.3 = (bf16[4,72,4608]{2,1,0:T(8,128)(2,1)}, bf16[4,72,4608]{2,1,0:T(8,128)(2,1)}, u32[]{:S(2)}, u32[]{:S(2)}) collective-permute-start(bf16[4,72,4608]{2,1,0:T(8,128)(2,1)} %get-tuple-element.20.refs_0_), channel_id=1, source_target_pairs={{0,6},{1,25},{2,0},{3,27},{4,2},{5,29},{6,4},{7,31},{8,14},{9,1},{... | collective-permute-start | bytes 7962632 | tf_op jit(solution)/shard_map/ppermute | solution.py:548
  287.8 1.6 copy-start
  287.8 35.2 %collective-permute-start.12 = (bf16[4,72,4608]{2,1,0:T(8,128)(2,1)S(1)}, bf16[4,72,4608]{2,1,0:T(8,128)(2,1)S(1)}, u32[]{:S(2)}, u32[]{:S(2)}) collective-permute-start(bf16[4,72,4608]{2,1,0:T(8,128)(2,1)S(1)} %collective-permute-done.7.refs_1_), channel_id=1, source_target_pairs={{0,1},{1,0},{2,3},{3,2},{4,5},{5,4},{6,7},{7,6},{8,9},{9,8},{10,11... | collective-permute-start | bytes 7962632 | tf_op jit(solution)/shard_map/ppermute | solution.py:548
  289.4 55.3 %collective-permute-start.8 = (bf16[4,72,4608]{2,1,0:T(8,128)(2,1)S(1)}, bf16[4,72,4608]{2,1,0:T(8,128)(2,1)}, u32[]{:S(2)}, u32[]{:S(2)}) collective-permute-start(bf16[4,72,4608]{2,1,0:T(8,128)(2,1)S(1)} %collective-permute-done.7.refs_1_), channel_id=1, source_target_pairs={{0,6},{1,25},{2,0},{3,27},{4,2},{5,29},{6,4},{7,31},{8,14},{9,1},{... | collective-permute-start | bytes 7962632 | tf_op jit(solution)/shard_map/ppermute | solution.py:548
  316.7 32.7 %collective-permute-start.1 = (bf16[4,72,4608]{2,1,0:T(8,128)(2,1)}, bf16[4,72,4608]{2,1,0:T(8,128)(2,1)}, u32[]{:S(2)}, u32[]{:S(2)}) collective-permute-start(bf16[4,72,4608]{2,1,0:T(8,128)(2,1)} %collective-permute-done.refs_0_), channel_id=1, source_target_pairs={{0,2},{1,9},{2,4},{3,11},{4,6},{5,13},{6,0},{7,15},{8,10},{9,17},{... | collective-permute-start | bytes 7962632 | tf_op jit(solution)/shard_map/ppermute | solution.py:548
  316.7 29.1 %copy-start.3 = (bf16[4,72,4608]{2,1,0:T(8,128)(2,1)}, bf16[4,72,4608]{2,1,0:T(8,128)(2,1)S(1)}, u32[]{:S(2)}) copy-start(bf16[4,72,4608]{2,1,0:T(8,128)(2,1)S(1)} %collective-permute-done.6.refs_1_) | copy-start | bytes 7962628
  316.7 4.0 collective-permute-start.16
  318.1 4.6 %collective-permute-start.19 = (bf16[4,144,1152]{2,1,0:T(8,128)(2,1)S(1)}, bf16[4,144,1152]{2,1,0:T(8,128)(2,1)S(1)}, u32[]{:S(2)}, u32[]{:S(2)}) collective-permute-start(bf16[4,144,1152]{2,1,0:T(8,128)(2,1)S(1)} %collective-permute-done.18.refs_1_), channel_id=1, source_target_pairs={{0,1},{1,0},{2,3},{3,2},{4,5},{5,4},{6,7},{7,6},{8,9},{9,8},{10,11... | collective-permute-start | bytes 3981320 | tf_op jit(solution)/shard_map/ppermute | solution.py:548
  320.7 30.8 %copy-start.16 = (bf16[4,144,1152]{2,1,0:T(8,128)(2,1)}, bf16[4,144,1152]{2,1,0:T(8,128)(2,1)S(1)}, u32[]{:S(2)}) copy-start(bf16[4,144,1152]{2,1,0:T(8,128)(2,1)S(1)} %collective-permute-done.16.refs_0_) | copy-start | bytes 3981316
  320.7 67.9 %collective-permute-start.11 = (bf16[4,72,4608]{2,1,0:T(8,128)(2,1)}, bf16[4,72,4608]{2,1,0:T(8,128)(2,1)}, u32[]{:S(2)}, u32[]{:S(2)}) collective-permute-start(bf16[4,72,4608]{2,1,0:T(8,128)(2,1)} %collective-permute-done.10.refs_0_), channel_id=1, source_target_pairs={{0,1},{1,0},{2,3},{3,2},{4,5},{5,4},{6,7},{7,6},{8,9},{9,8},{10,11... | collective-permute-start | bytes 7962632 | tf_op jit(solution)/shard_map/ppermute | solution.py:548
  322.6 28.9 %copy-start.17 = (bf16[4,144,1152]{2,1,0:T(8,128)(2,1)}, bf16[4,144,1152]{2,1,0:T(8,128)(2,1)S(1)}, u32[]{:S(2)}) copy-start(bf16[4,144,1152]{2,1,0:T(8,128)(2,1)S(1)} %collective-permute-done.19.refs_1_) | copy-start | bytes 3981316
  322.6 74.2 %collective-permute-start.4 = (bf16[4,72,4608]{2,1,0:T(8,128)(2,1)}, bf16[4,72,4608]{2,1,0:T(8,128)(2,1)}, u32[]{:S(2)}, u32[]{:S(2)}) collective-permute-start(bf16[4,72,4608]{2,1,0:T(8,128)(2,1)} %collective-permute-done.refs_0_), channel_id=1, source_target_pairs={{0,1},{1,0},{2,3},{3,2},{4,5},{5,4},{6,7},{7,6},{8,9},{9,8},{10,11... | collective-permute-start | bytes 7962632 | tf_op jit(solution)/shard_map/ppermute | solution.py:548
  323.0 21.7 %copy-start.1 = (bf16[4,72,4608]{2,1,0:T(8,128)(2,1)}, bf16[4,72,4608]{2,1,0:T(8,128)(2,1)S(1)}, u32[]{:S(2)}) copy-start(bf16[4,72,4608]{2,1,0:T(8,128)(2,1)S(1)} %collective-permute-done.12.refs_3_) | copy-start | bytes 7962628
  323.0 73.9 %collective-permute-start.5 = (bf16[4,72,4608]{2,1,0:T(8,128)(2,1)}, bf16[4,72,4608]{2,1,0:T(8,128)(2,1)}, u32[]{:S(2)}, u32[]{:S(2)}) collective-permute-start(bf16[4,72,4608]{2,1,0:T(8,128)(2,1)} %collective-permute-done.3.refs_1_), channel_id=1, source_target_pairs={{0,1},{1,0},{2,3},{3,2},{4,5},{5,4},{6,7},{7,6},{8,9},{9,8},{10,11... | collective-permute-start | bytes 7962632 | tf_op jit(solution)/shard_map/ppermute | solution.py:548
  344.7 60.4 %collective-permute-start.9 = (bf16[4,72,4608]{2,1,0:T(8,128)(2,1)}, bf16[4,72,4608]{2,1,0:T(8,128)(2,1)}, u32[]{:S(2)}, u32[]{:S(2)}) collective-permute-start(bf16[4,72,4608]{2,1,0:T(8,128)(2,1)} %collective-permute-done.8.refs_0_), channel_id=1, source_target_pairs={{0,1},{1,0},{2,3},{3,2},{4,5},{5,4},{6,7},{7,6},{8,9},{9,8},{10,11... | collective-permute-start | bytes 7962632 | tf_op jit(solution)/shard_map/ppermute | solution.py:548
  349.4 60.0 %collective-permute-start.2 = (bf16[4,72,4608]{2,1,0:T(8,128)(2,1)}, bf16[4,72,4608]{2,1,0:T(8,128)(2,1)}, u32[]{:S(2)}, u32[]{:S(2)}) collective-permute-start(bf16[4,72,4608]{2,1,0:T(8,128)(2,1)} %collective-permute-done.1.refs_0_), channel_id=1, source_target_pairs={{0,1},{1,0},{2,3},{3,2},{4,5},{5,4},{6,7},{7,6},{8,9},{9,8},{10,11... | collective-permute-start | bytes 7962632 | tf_op jit(solution)/shard_map/ppermute | solution.py:548
